TPU v7x, 1024 devices: a whole 8x8x8 slice. The times are simulated.
1024 devices in a mesh: wide: 32 (over y, z_lo), fields: 32 (over x, z_hi, core).
Axes of the slice: x: 8, y: 8, z: 8 (z_hi: 2, z_lo: 4; z = z_hi * 4 + z_lo), core: 2. Of those that a mesh axis runs over, the one named last changes fastest.
Arguments:
- vectors: float32 [1024, 16384], P('wide', 'fields'), may hold values from 0.03 to 82, as said below
- pivot_ids: int32 [8], replicated, may hold values from 0 to 1023
Outputs:
- similarity: float32 [1024, 4, 256], P('wide', None, 'fields')
Inputs may be any that keep to these rules, and one draw needn't show every extreme that they name: `vectors`: every entry is positive.
All inputs are finite; a program needn't handle non-finite values.
Results may differ from a plain program's by a relative error of at most 0.0003.
Values sent between devices are 32-bit elements; how exact they have to be, the bound alone decides.
No kernel may reach another device: no remote copies, remote signals or barrier semaphores. Data moves between devices by JAX's collectives and lax.ppermute only.
A program may use at most 32 MiB of HBM per device.

v0:
```python
import jax
import jax.numpy as jnp
from jax import lax
from jax.sharding import PartitionSpec as P

STEPS = 4


def from_everyone(array, axis):
    copies = jnp.broadcast_to(array, (lax.axis_size(axis), *array.shape))
    return lax.all_to_all(copies, axis, split_axis=0, concat_axis=0, tiled=True)


def over_copies(array, axis):
    return from_everyone(array, axis).sum(axis=0)


def together(arrays, axis):
    flat, at, finished = (jnp.concatenate([a.reshape(-1) for a in arrays]), 0, [])
    so_far = over_copies(flat, axis)
    for a in arrays:
        finished.append(so_far[at : at + a.size].reshape(a.shape))
        at += a.size
    return tuple(finished)


def from_behind(value, axis, steps):
    count = lax.axis_size(axis)
    pairs = [(source, (source + steps) % count) for source in range(count)]
    return lax.ppermute(value, axis, pairs)


def cut_along(array, dim, peers):
    shape = array.shape
    tiles = array.reshape(*shape[:dim], peers, shape[dim] // peers, *shape[dim + 1 :])
    return jnp.moveaxis(tiles, dim, 0)


def sum_at_owner(array, axis, dim):
    tiles = cut_along(array, dim, lax.axis_size(axis))
    arrived = lax.all_to_all(tiles, axis, split_axis=0, concat_axis=0, tiled=True)
    return arrived.sum(axis=0)


def triple_table(owned, pivots, minima, partner):
    with_pivot = jnp.sum(minima, axis=-1)
    pivot_side = jnp.sum(jnp.minimum(pivots[:, None, :], partner[None, :, :]), axis=-1)
    pair_side = jnp.sum(jnp.minimum(owned[:, None, :], partner[None, :, :]), axis=-1)
    triple = lax.map(
        lambda layer: jnp.sum(jnp.minimum(layer[:, None, :], partner[None, :, :]), axis=-1),
        jnp.transpose(minima, (1, 0, 2)),
    )
    return (
        with_pivot[:, :, None]
        + pivot_side[None, :, :]
        + pair_side[:, None, :]
        - jnp.transpose(triple, (1, 0, 2))
    )


def body(vectors, pivot_ids):
    row_count = vectors.shape[0]
    pivot_count = pivot_ids.shape[0]
    first_row = lax.axis_index("wide") * row_count
    chosen = (
        pivot_ids[:, None] == first_row + jnp.arange(row_count, dtype=jnp.int32)[None, :]
    ).astype(jnp.float32)
    pivot_part = jnp.dot(
        chosen, vectors, precision=lax.Precision.HIGHEST, preferred_element_type=jnp.float32
    )
    pivots = over_copies(pivot_part, "wide")
    owned_total, pivot_total = together(
        (jnp.sum(vectors, axis=1), jnp.sum(pivots, axis=1)), "fields"
    )
    minima = jnp.minimum(vectors[:, None, :], pivots[None, :, :])
    partner, partner_total = (vectors, owned_total)
    numerators = []
    partner_totals = []
    for stride in range(1, STEPS + 1):
        partner, partner_total = from_behind((partner, partner_total), "wide", 1)
        partner_totals.append(partner_total)
        numerator = triple_table(vectors, pivots, minima, partner).reshape(
            row_count, pivot_count * row_count
        )
        numerators.append(numerator)
    stacked = jnp.stack(numerators, axis=1)
    shares = sum_at_owner(stacked, "fields", 2)
    share_width = shares.shape[2]
    offset = lax.axis_index("fields") * share_width
    step_totals = jnp.stack(partner_totals, axis=0)
    denominator = (
        owned_total[:, None, None, None]
        + pivot_total[None, None, :, None]
        + step_totals[None, :, None, :]
    )
    denominator = denominator.reshape(row_count, STEPS, pivot_count * row_count)
    denominator = lax.dynamic_slice_in_dim(denominator, offset, share_width, 2)
    return 1.5 * shares / denominator


def solution(mesh):
    placed = (P("wide", "fields"), P())
    return jax.shard_map(
        body, mesh=mesh, in_specs=placed, out_specs=P("wide", None, "fields"), check_vma=False
    )
```

profile of v0, /device:TPU:2, one launch (start us, length us, event | category | flops | bytes accessed | tf_op | source)
XLA Modules:
  0.0 146.8 jit_solution(18065481417415474425)
XLA Ops:
  0.0 1.0 fusion
  1.1 0.9 broadcast_in_dim.19
  1.9 16.2 %all-to-all-start = ((f32[32,8,512]{2,1,0:T(8,128)}), f32[32,8,512]{2,1,0:T(8,128)S(1)}, u32[]{:S(2)}, u32[]{:S(2)}) async-start(f32[32,8,512]{2,1,0:T(8,128)} %broadcast_in_dim.19), calls=%async_computation | async-start | bytes 1048576 | tf_op jit(solution)/shard_map/all_to_all | solution.py:11
  18.2 3.7 %collective-permute-start = (f32[32,512]{1,0:T(8,128)S(1)}, f32[32,512]{1,0:T(8,128)S(1)}, u32[]{:S(2)}, u32[]{:S(2)}) collective-permute-start(f32[32,512]{1,0:T(8,128)S(1)} %copy-done), channel_id=1, source_target_pairs={{0,32},{32,64},{64,96},{96,128},{128,160},{160,192},{192,224},{224... | collective-permute-start | bytes 196616 | tf_op jit(solution)/shard_map/ppermute | solution.py:30
  21.9 14.5 %collective-permute-done = f32[32,512]{1,0:T(8,128)S(1)} collective-permute-done((f32[32,512]{1,0:T(8,128)S(1)}, f32[32,512]{1,0:T(8,128)S(1)}, u32[]{:S(2)}, u32[]{:S(2)}) %collective-permute-start) | collective-permute-done | bytes 65568 | tf_op jit(solution)/shard_map/ppermute | solution.py:30
  36.4 1.9 %collective-permute-start.1 = (f32[32,512]{1,0:T(8,128)S(1)}, f32[32,512]{1,0:T(8,128)S(1)}, u32[]{:S(2)}, u32[]{:S(2)}) collective-permute-start(f32[32,512]{1,0:T(8,128)S(1)} %collective-permute-done), channel_id=1, source_target_pairs={{0,32},{32,64},{64,96},{96,128},{128,160},{160,192},{192,224},{224... | collective-permute-start | bytes 196616 | tf_op jit(solution)/shard_map/ppermute | solution.py:30
  38.3 8.1 %collective-permute-done.1 = f32[32,512]{1,0:T(8,128)S(1)} collective-permute-done((f32[32,512]{1,0:T(8,128)S(1)}, f32[32,512]{1,0:T(8,128)S(1)}, u32[]{:S(2)}, u32[]{:S(2)}) %collective-permute-start.1) | collective-permute-done | bytes 65568 | tf_op jit(solution)/shard_map/ppermute | solution.py:30
  46.4 1.9 %collective-permute-start.2 = (f32[32,512]{1,0:T(8,128)S(1)}, f32[32,512]{1,0:T(8,128)S(1)}, u32[]{:S(2)}, u32[]{:S(2)}) collective-permute-start(f32[32,512]{1,0:T(8,128)S(1)} %collective-permute-done.1), channel_id=1, source_target_pairs={{0,32},{32,64},{64,96},{96,128},{128,160},{160,192},{192,224},{224... | collective-permute-start | bytes 196616 | tf_op jit(solution)/shard_map/ppermute | solution.py:30
  48.4 8.1 %collective-permute-done.2 = f32[32,512]{1,0:T(8,128)S(1)} collective-permute-done((f32[32,512]{1,0:T(8,128)S(1)}, f32[32,512]{1,0:T(8,128)S(1)}, u32[]{:S(2)}, u32[]{:S(2)}) %collective-permute-start.2) | collective-permute-done | bytes 65568 | tf_op jit(solution)/shard_map/ppermute | solution.py:30
  56.5 1.9 %collective-permute-start.3 = (f32[32,512]{1,0:T(8,128)S(1)}, f32[32,512]{1,0:T(8,128)S(1)}, u32[]{:S(2)}, u32[]{:S(2)}) collective-permute-start(f32[32,512]{1,0:T(8,128)S(1)} %collective-permute-done.2), channel_id=1, source_target_pairs={{0,32},{32,64},{64,96},{96,128},{128,160},{160,192},{192,224},{224... | collective-permute-start | bytes 196616 | tf_op jit(solution)/shard_map/ppermute | solution.py:30
  58.5 8.0 %collective-permute-done.3 = f32[32,512]{1,0:T(8,128)S(1)} collective-permute-done((f32[32,512]{1,0:T(8,128)S(1)}, f32[32,512]{1,0:T(8,128)S(1)}, u32[]{:S(2)}, u32[]{:S(2)}) %collective-permute-start.3) | collective-permute-done | bytes 65568 | tf_op jit(solution)/shard_map/ppermute | solution.py:30
  66.6 0.7 minimum_reduce_fusion.7
  68.2 2.5 %while.40 = (s32[]{:T(128)}, f32[8,32,32]{1,2,0:T(8,128)S(1)}, f32[8,32,512]{2,1,0:T(8,128)S(1)}, f32[32,512]{1,0:T(8,128)S(1)}, s32[]{:T(128)}) while((s32[]{:T(128)}, f32[8,32,32]{1,2,0:T(8,128)S(1)}, f32[8,32,512]{2,1,0:T(8,128)S(1)}, f32[32,512]{1,0:T(8,128)S(1)}, s32[]{:T(128)}) %tuple.68), condition=%wide.region_6.0_spmd, body=%wide.region_4.6_spmd.sunk | while | flops 1047554 | bytes 307277 | solution.py:49
  70.8 2.5 %while.41 = (s32[]{:T(128)}, f32[8,32,32]{1,2,0:T(8,128)S(1)}, f32[8,32,512]{2,1,0:T(8,128)S(1)}, f32[32,512]{1,0:T(8,128)S(1)}, s32[]{:T(128)}) while((s32[]{:T(128)}, f32[8,32,32]{1,2,0:T(8,128)S(1)}, f32[8,32,512]{2,1,0:T(8,128)S(1)}, f32[32,512]{1,0:T(8,128)S(1)}, s32[]{:T(128)}) %tuple.80), condition=%wide.region_11.12_spmd, body=%wide.region_9.11_spmd.sunk | while | flops 1047554 | bytes 307277 | solution.py:49
  73.3 2.5 %while.42 = (s32[]{:T(128)}, f32[8,32,32]{1,2,0:T(8,128)S(1)}, f32[8,32,512]{2,1,0:T(8,128)S(1)}, f32[32,512]{1,0:T(8,128)S(1)}, s32[]{:T(128)}) while((s32[]{:T(128)}, f32[8,32,32]{1,2,0:T(8,128)S(1)}, f32[8,32,512]{2,1,0:T(8,128)S(1)}, f32[32,512]{1,0:T(8,128)S(1)}, s32[]{:T(128)}) %tuple.81), condition=%wide.region_16.17_spmd, body=%wide.region_14.0_spmd.sunk | while | flops 1047554 | bytes 307277 | solution.py:49
  75.8 2.5 %while.43 = (s32[]{:T(128)}, f32[8,32,32]{1,2,0:T(8,128)S(1)}, f32[8,32,512]{2,1,0:T(8,128)S(1)}, f32[32,512]{1,0:T(8,128)S(1)}, s32[]{:T(128)}) while((s32[]{:T(128)}, f32[8,32,32]{1,2,0:T(8,128)S(1)}, f32[8,32,512]{2,1,0:T(8,128)S(1)}, f32[32,512]{1,0:T(8,128)S(1)}, s32[]{:T(128)}) %tuple.82), condition=%wide.region_21.22_spmd, body=%wide.region_19.21_spmd.sunk | while | flops 1047554 | bytes 307277 | solution.py:49
  78.4 0.6 broadcast_in_dim.20
  79.0 16.8 %all-to-all-start.2 = ((f32[32,1,40]{2,1,0:T(1,128)}), f32[32,1,40]{2,1,0:T(1,128)S(1)}, u32[]{:S(2)}, u32[]{:S(2)}) async-start(f32[32,1,40]{2,1,0:T(1,128)} %broadcast_in_dim.20), calls=%async_computation.2 | async-start | bytes 32768 | tf_op jit(solution)/shard_map/all_to_all | solution.py:11
  96.1 10.7 %all-to-all-done.2 = f32[32,1,40]{2,1,0:T(1,128)S(1)} async-done(((f32[32,1,40]{2,1,0:T(1,128)}), f32[32,1,40]{2,1,0:T(1,128)S(1)}, u32[]{:S(2)}, u32[]{:S(2)}) %all-to-all-start.2) | async-done | bytes 5152 | tf_op jit(solution)/shard_map/all_to_all | solution.py:11
  106.8 1.9 %collective-permute-start.4 = (f32[32]{0:T(128)S(1)}, f32[32]{0:T(128)S(1)}, u32[]{:S(2)}, u32[]{:S(2)}) collective-permute-start(f32[32]{0:T(128)S(1)} %bitcast.65), channel_id=1, source_target_pairs={{0,32},{32,64},{64,96},{96,128},{128,160},{160,192},{192,224},{224... | collective-permute-start | bytes 392 | tf_op jit(solution)/shard_map/ppermute | solution.py:30
  108.8 0.9 reshape.82
  109.7 6.5 %collective-permute-done.4 = f32[32]{0:T(128)S(1)} collective-permute-done((f32[32]{0:T(128)S(1)}, f32[32]{0:T(128)S(1)}, u32[]{:S(2)}, u32[]{:S(2)}) %collective-permute-start.4) | collective-permute-done | bytes 160 | tf_op jit(solution)/shard_map/ppermute | solution.py:30
  116.2 1.9 %collective-permute-start.5 = (f32[32]{0:T(128)S(1)}, f32[32]{0:T(128)S(1)}, u32[]{:S(2)}, u32[]{:S(2)}) collective-permute-start(f32[32]{0:T(128)S(1)} %collective-permute-done.4), channel_id=1, source_target_pairs={{0,32},{32,64},{64,96},{96,128},{128,160},{160,192},{192,224},{224... | collective-permute-start | bytes 392 | tf_op jit(solution)/shard_map/ppermute | solution.py:30
  118.1 4.9 %all-to-all-start.1 = ((f32[32,1,1024]{2,1,0:T(1,128)}), f32[32,1,1024]{2,1,0:T(1,128)S(1)}, u32[]{:S(2)}, u32[]{:S(2)}) async-start(f32[32,1,1024]{2,1,0:T(1,128)} %reshape.82), calls=%async_computation.1 | async-start | bytes 262144 | tf_op jit(solution)/shard_map/all_to_all | solution.py:41
  123.1 2.4 %collective-permute-done.5 = f32[32]{0:T(128)S(1)} collective-permute-done((f32[32]{0:T(128)S(1)}, f32[32]{0:T(128)S(1)}, u32[]{:S(2)}, u32[]{:S(2)}) %collective-permute-start.5) | collective-permute-done | bytes 160 | tf_op jit(solution)/shard_map/ppermute | solution.py:30
  125.5 1.9 %collective-permute-start.6 = (f32[32]{0:T(128)S(1)}, f32[32]{0:T(128)S(1)}, u32[]{:S(2)}, u32[]{:S(2)}) collective-permute-start(f32[32]{0:T(128)S(1)} %collective-permute-done.5), channel_id=1, source_target_pairs={{0,32},{32,64},{64,96},{96,128},{128,160},{160,192},{192,224},{224... | collective-permute-start | bytes 392 | tf_op jit(solution)/shard_map/ppermute | solution.py:30
  127.5 7.4 %collective-permute-done.6 = f32[32]{0:T(128)S(1)} collective-permute-done((f32[32]{0:T(128)S(1)}, f32[32]{0:T(128)S(1)}, u32[]{:S(2)}, u32[]{:S(2)}) %collective-permute-start.6) | collective-permute-done | bytes 160 | tf_op jit(solution)/shard_map/ppermute | solution.py:30
  134.9 1.9 %collective-permute-start.7 = (f32[32]{0:T(128)S(1)}, f32[32]{0:T(128)S(1)}, u32[]{:S(2)}, u32[]{:S(2)}) collective-permute-start(f32[32]{0:T(128)S(1)} %collective-permute-done.6), channel_id=1, source_target_pairs={{0,32},{32,64},{64,96},{96,128},{128,160},{160,192},{192,224},{224... | collective-permute-start | bytes 392 | tf_op jit(solution)/shard_map/ppermute | solution.py:30
  136.8 7.4 %collective-permute-done.7 = f32[32]{0:T(128)S(1)} collective-permute-done((f32[32]{0:T(128)S(1)}, f32[32]{0:T(128)S(1)}, u32[]{:S(2)}, u32[]{:S(2)}) %collective-permute-start.7) | collective-permute-done | bytes 160 | tf_op jit(solution)/shard_map/ppermute | solution.py:30
  144.4 0.5 broadcast.62
  144.9 0.9 reduce.2
  146.1 0.7 add_divide_fusion
  (160 shorter events, 11.7 us)
Async XLA Ops:
  1.9 16.2 %copy-start = (f32[32,512]{1,0:T(8,128)S(1)}, f32[32,512]{1,0:T(8,128)}, u32[]{:S(2)}) copy-start(f32[32,512]{1,0:T(8,128)} %param.10) | copy-start | bytes 196612
  1.9 65.6 %all-to-all-start = ((f32[32,8,512]{2,1,0:T(8,128)}), f32[32,8,512]{2,1,0:T(8,128)S(1)}, u32[]{:S(2)}, u32[]{:S(2)}) async-start(f32[32,8,512]{2,1,0:T(8,128)} %broadcast_in_dim.19), calls=%async_computation | async-start | bytes 1048576 | tf_op jit(solution)/shard_map/all_to_all | solution.py:11
  18.2 18.2 %collective-permute-start = (f32[32,512]{1,0:T(8,128)S(1)}, f32[32,512]{1,0:T(8,128)S(1)}, u32[]{:S(2)}, u32[]{:S(2)}) collective-permute-start(f32[32,512]{1,0:T(8,128)S(1)} %copy-done), channel_id=1, source_target_pairs={{0,32},{32,64},{64,96},{96,128},{128,160},{160,192},{192,224},{224... | collective-permute-start | bytes 196616 | tf_op jit(solution)/shard_map/ppermute | solution.py:30
  36.4 10.1 %collective-permute-start.1 = (f32[32,512]{1,0:T(8,128)S(1)}, f32[32,512]{1,0:T(8,128)S(1)}, u32[]{:S(2)}, u32[]{:S(2)}) collective-permute-start(f32[32,512]{1,0:T(8,128)S(1)} %collective-permute-done), channel_id=1, source_target_pairs={{0,32},{32,64},{64,96},{96,128},{128,160},{160,192},{192,224},{224... | collective-permute-start | bytes 196616 | tf_op jit(solution)/shard_map/ppermute | solution.py:30
  46.4 10.1 %collective-permute-start.2 = (f32[32,512]{1,0:T(8,128)S(1)}, f32[32,512]{1,0:T(8,128)S(1)}, u32[]{:S(2)}, u32[]{:S(2)}) collective-permute-start(f32[32,512]{1,0:T(8,128)S(1)} %collective-permute-done.1), channel_id=1, source_target_pairs={{0,32},{32,64},{64,96},{96,128},{128,160},{160,192},{192,224},{224... | collective-permute-start | bytes 196616 | tf_op jit(solution)/shard_map/ppermute | solution.py:30
  56.5 10.1 %collective-permute-start.3 = (f32[32,512]{1,0:T(8,128)S(1)}, f32[32,512]{1,0:T(8,128)S(1)}, u32[]{:S(2)}, u32[]{:S(2)}) collective-permute-start(f32[32,512]{1,0:T(8,128)S(1)} %collective-permute-done.2), channel_id=1, source_target_pairs={{0,32},{32,64},{64,96},{96,128},{128,160},{160,192},{192,224},{224... | collective-permute-start | bytes 196616 | tf_op jit(solution)/shard_map/ppermute | solution.py:30
  79.0 27.8 %all-to-all-start.2 = ((f32[32,1,40]{2,1,0:T(1,128)}), f32[32,1,40]{2,1,0:T(1,128)S(1)}, u32[]{:S(2)}, u32[]{:S(2)}) async-start(f32[32,1,40]{2,1,0:T(1,128)} %broadcast_in_dim.20), calls=%async_computation.2 | async-start | bytes 32768 | tf_op jit(solution)/shard_map/all_to_all | solution.py:11
  106.8 9.4 %collective-permute-start.4 = (f32[32]{0:T(128)S(1)}, f32[32]{0:T(128)S(1)}, u32[]{:S(2)}, u32[]{:S(2)}) collective-permute-start(f32[32]{0:T(128)S(1)} %bitcast.65), channel_id=1, source_target_pairs={{0,32},{32,64},{64,96},{96,128},{128,160},{160,192},{192,224},{224... | collective-permute-start | bytes 392 | tf_op jit(solution)/shard_map/ppermute | solution.py:30
  116.2 9.4 %collective-permute-start.5 = (f32[32]{0:T(128)S(1)}, f32[32]{0:T(128)S(1)}, u32[]{:S(2)}, u32[]{:S(2)}) collective-permute-start(f32[32]{0:T(128)S(1)} %collective-permute-done.4), channel_id=1, source_target_pairs={{0,32},{32,64},{64,96},{96,128},{128,160},{160,192},{192,224},{224... | collective-permute-start | bytes 392 | tf_op jit(solution)/shard_map/ppermute | solution.py:30
  118.1 26.3 %all-to-all-start.1 = ((f32[32,1,1024]{2,1,0:T(1,128)}), f32[32,1,1024]{2,1,0:T(1,128)S(1)}, u32[]{:S(2)}, u32[]{:S(2)}) async-start(f32[32,1,1024]{2,1,0:T(1,128)} %reshape.82), calls=%async_computation.1 | async-start | bytes 262144 | tf_op jit(solution)/shard_map/all_to_all | solution.py:41
  125.5 9.4 %collective-permute-start.6 = (f32[32]{0:T(128)S(1)}, f32[32]{0:T(128)S(1)}, u32[]{:S(2)}, u32[]{:S(2)}) collective-permute-start(f32[32]{0:T(128)S(1)} %collective-permute-done.5), channel_id=1, source_target_pairs={{0,32},{32,64},{64,96},{96,128},{128,160},{160,192},{192,224},{224... | collective-permute-start | bytes 392 | tf_op jit(solution)/shard_map/ppermute | solution.py:30
  134.9 9.4 %collective-permute-start.7 = (f32[32]{0:T(128)S(1)}, f32[32]{0:T(128)S(1)}, u32[]{:S(2)}, u32[]{:S(2)}) collective-permute-start(f32[32]{0:T(128)S(1)} %collective-permute-done.6), channel_id=1, source_target_pairs={{0,32},{32,64},{64,96},{96,128},{128,160},{160,192},{192,224},{224... | collective-permute-start | bytes 392 | tf_op jit(solution)/shard_map/ppermute | solution.py:30
where the time goes:
time: 147 us
  waiting for transfers between devices  73.2 us (50%)
  starting transfers between devices  55.1 us (37%)
  other arithmetic  10.5 us (7%)
  local copies, waits for them, and re-layouts  6.36 us (4%)
    ppermute x8, waiting for transfers between devices, from_behind(): return lax.ppermute(value, axis, pairs)  62.5 us
    all_to_all x2, starting transfers between devices, from_everyone(): return lax.all_to_all(copies, axis, split_axis=0, concat_axis=0, tiled=True)  33.1 us
    ppermute x8, starting transfers between devices, from_behind(): return lax.ppermute(value, axis, pairs)  17.1 us
    all_to_all x2, waiting for transfers between devices, from_everyone(): return lax.all_to_all(copies, axis, split_axis=0, concat_axis=0, tiled=True)  10.7 us
    reduce_sum x32, other arithmetic, triple_table(): jnp.sum(jnp.minimum(layer[:, None, :], partner[None, :, :]), axis=-1)  6.96 us
    all_to_all x1, starting transfers between devices, sum_at_owner(): lax.all_to_all(tiles, axis, split_axis=0, concat_axis=0, tiled=True)  4.93 us
  transfers between devices with their start and end apart: 11, of which 9 were waited for; matrix products, arithmetic and copies ran while one was open for 2% of the time, Pallas kernels for 0%

commit v1 on v0

v1 whole, which is shorter than its diff:
```python
import jax
import jax.numpy as jnp
from jax import lax
from jax.experimental import pallas as pl
from jax.experimental.pallas import tpu as pltpu
from jax.sharding import PartitionSpec as P

STEPS = 4
LANES = 128
SUBLANES = 8
SHARE_ROWS = SUBLANES + 1


def from_behind(value, axis, steps):
    count = lax.axis_size(axis)
    pairs = [(source, (source + steps) % count) for source in range(count)]
    return lax.ppermute(value, axis, pairs)


def to_everyone(copies, axis):
    return lax.all_to_all(copies, axis, split_axis=0, concat_axis=0, tiled=True)


def spread_kernel(ids_ref, vectors_ref, copies_ref, rows_ref):
    row_count = vectors_ref.shape[0]
    for q in range(rows_ref.shape[0]):
        rows_ref[q : q + 1, :] = vectors_ref[pl.ds(lax.rem(ids_ref[q], row_count), 1), :]
    rows = rows_ref[...]
    for peer in range(copies_ref.shape[0]):
        copies_ref[peer] = rows


def lane_at(offset):
    lane = lax.broadcasted_iota(jnp.int32, (SUBLANES, LANES), 1)
    sublane = lax.broadcasted_iota(jnp.int32, (SUBLANES, LANES), 0)
    return lane == sublane + offset


def column_sum(tiles):
    folded = tiles[0]
    for tile in tiles[1:]:
        folded = folded + tile
    return jnp.sum(folded, axis=1, keepdims=True)


def row_of(columns):
    row = jnp.zeros((SUBLANES, LANES), jnp.float32)
    for offset, column in columns:
        row = row + jnp.where(lane_at(offset), column, 0.0)
    return jnp.sum(row, axis=0, keepdims=True)


def table_kernel(ids_ref, own_ref, arrived_ref, *refs):
    partner_refs = refs[:STEPS]
    out_ref, pivots_ref, larger_ref = refs[STEPS:]
    row_count, width = own_ref.shape
    pivot_count = pivots_ref.shape[0]
    tiles = width // LANES
    v_tiles = row_count // SUBLANES
    q_lanes = LANES // row_count
    q_tiles = pivot_count // q_lanes
    for q in range(pivot_count):
        pivots_ref[q : q + 1, :] = arrived_ref[lax.div(ids_ref[q], row_count), q : q + 1, :]

    smaller = []
    for qt in range(q_tiles):
        columns = []
        for ql in range(q_lanes):
            q = qt * q_lanes + ql
            for vt in range(v_tiles):
                low = [
                    jnp.minimum(
                        own_ref[vt * SUBLANES : (vt + 1) * SUBLANES, t * LANES : (t + 1) * LANES],
                        pivots_ref[q : q + 1, t * LANES : (t + 1) * LANES],
                    )
                    for t in range(tiles)
                ]
                columns.append((ql * row_count + vt * SUBLANES, column_sum(low)))
        smaller.append(row_of(columns))
        for t in range(tiles):
            at = slice(t * LANES, (t + 1) * LANES)
            high = jnp.concatenate(
                [
                    jnp.maximum(own_ref[:, at], pivots_ref[qt * q_lanes + ql : qt * q_lanes + ql + 1, at])
                    for ql in range(q_lanes)
                ],
                axis=0,
            )
            larger_ref[qt, at, :] = high.T

    def some_fields(t, sums):
        at = pl.ds(t * LANES, LANES)
        blocks = [
            ref[vt * SUBLANES : (vt + 1) * SUBLANES, at] for ref in partner_refs for vt in range(v_tiles)
        ]
        sums = list(sums)
        for f in range(LANES):
            rows = [
                jnp.broadcast_to(larger_ref[qt, pl.ds(t * LANES + f, 1), :], (SUBLANES, LANES))
                for qt in range(q_tiles)
            ]
            for i, block in enumerate(blocks):
                x = jnp.broadcast_to(block[:, f : f + 1], (SUBLANES, LANES))
                for qt in range(q_tiles):
                    k = i * q_tiles + qt
                    sums[k] = sums[k] + jnp.minimum(x, rows[qt])
        return tuple(sums)

    first = tuple(
        jnp.broadcast_to(smaller[k % q_tiles], (SUBLANES, LANES))
        for k in range(STEPS * v_tiles * q_tiles)
    )
    sums = lax.fori_loop(0, tiles, some_fields, first)

    for vt in range(v_tiles):
        for q in range(pivot_count):
            qt, ql = divmod(q, q_lanes)
            lanes = slice(ql * row_count, (ql + 1) * row_count)
            tile = jnp.concatenate(
                [sums[(s * v_tiles + vt) * q_tiles + qt][:, lanes] for s in range(STEPS)], axis=1
            )
            at = (q * v_tiles + vt) * SHARE_ROWS
            out_ref[at : at + SUBLANES, :] = tile

    def totals(ref, vt):
        rows = slice(vt * SUBLANES, (vt + 1) * SUBLANES)
        return column_sum([ref[rows, t * LANES : (t + 1) * LANES] for t in range(tiles)])

    pivot_total = totals(pivots_ref, 0)
    own_row = row_of([(vt * SUBLANES, totals(own_ref, vt)) for vt in range(v_tiles)])
    lane = lax.broadcasted_iota(jnp.int32, (SUBLANES, LANES), 1)
    for vt in range(v_tiles):
        partner_row = row_of(
            [(row_count + s * SUBLANES, totals(partner_refs[s], vt)) for s in range(STEPS)]
        )
        rows = jnp.where(lane < row_count, own_row + pivot_total, partner_row)
        for q in range(pivot_count):
            at = (q * v_tiles + vt) * SHARE_ROWS + SUBLANES
            out_ref[at : at + 1, :] = rows[q : q + 1, :]


def quotient_kernel(arrived_ref, out_ref):
    steps, _, row_count = out_ref.shape
    peers = arrived_ref.shape[0] // SHARE_ROWS
    numerator = arrived_ref[0:SUBLANES, :]
    total = arrived_ref[SUBLANES : SUBLANES + 1, :]
    for peer in range(1, peers):
        at = peer * SHARE_ROWS
        numerator = numerator + arrived_ref[at : at + SUBLANES, :]
        total = total + arrived_ref[at + SUBLANES : at + SUBLANES + 1, :]
    totals = jnp.broadcast_to(total, (SUBLANES, LANES))
    for s in range(steps):
        partner = jnp.sum(
            jnp.where(lane_at(row_count + s * SUBLANES), totals, 0.0), axis=1, keepdims=True
        )
        own = totals[:, :row_count]
        part = numerator[:, s * row_count : (s + 1) * row_count]
        out_ref[s] = 1.5 * part / (own + partner)


def in_vmem(array):
    return pltpu.with_memory_space_constraint(array, pltpu.VMEM)


def body(vectors, pivot_ids):
    row_count, width = vectors.shape
    pivot_count = pivot_ids.shape[0]
    wide = lax.axis_size("wide")
    fields = lax.axis_size("fields")
    smem = pl.BlockSpec(memory_space=pltpu.SMEM)
    vmem = pl.BlockSpec(memory_space=pltpu.VMEM)
    copies = pl.pallas_call(
        spread_kernel,
        out_shape=pltpu.VMEM((wide, pivot_count, width), jnp.float32),
        in_specs=[smem, vmem],
        out_specs=vmem,
        scratch_shapes=[pltpu.VMEM((pivot_count, width), jnp.float32)],
        name="spread",
    )(pivot_ids, in_vmem(vectors))
    arrived = to_everyone(copies, "wide")
    partners = [from_behind(vectors, "wide", s) for s in range(1, STEPS + 1)]
    table = pl.pallas_call(
        table_kernel,
        out_shape=pltpu.VMEM((fields * SHARE_ROWS, LANES), jnp.float32),
        in_specs=[smem] + [vmem] * (2 + STEPS),
        out_specs=vmem,
        scratch_shapes=[
            pltpu.VMEM((pivot_count, width), jnp.float32),
            pltpu.VMEM((pivot_count * row_count // LANES, width, LANES), jnp.float32),
        ],
        name="table",
    )(pivot_ids, *(in_vmem(a) for a in (vectors, arrived, *partners)))
    shares = to_everyone(table.reshape(fields, 1, SHARE_ROWS * LANES), "fields")
    quotient = pl.pallas_call(
        quotient_kernel,
        out_shape=jax.ShapeDtypeStruct((STEPS, SUBLANES, row_count), jnp.float32),
        in_specs=[vmem],
        out_specs=vmem,
        name="quotient",
    )(in_vmem(shares.reshape(fields * SHARE_ROWS, LANES)))
    return jnp.transpose(quotient, (2, 0, 1))


def solution(mesh):
    placed = (P("wide", "fields"), P())
    return jax.shard_map(
        body, mesh=mesh, in_specs=placed, out_specs=P("wide", None, "fields"), check_vma=False
    )
```

time: 147 us -> 82.9 us (0.56)
  the two profiles are of different devices: /device:TPU:2 before, /device:TPU:1 now
where the time goes in v1:
time: 82.9 us; the launch traced here: 82.5 us
  blocking collectives  33.4 us (40%)
  starting transfers between devices  30.9 us (37%)
  Pallas kernels  13.8 us (17%)
  waiting for transfers between devices  3.59 us (4%)
  local copies, waits for them, and re-layouts  0.84 us (1%)
    all_to_all x1, blocking collectives, to_everyone(): return lax.all_to_all(copies, axis, split_axis=0, concat_axis=0, tiled=True)  33.4 us
    all_to_all x1, starting transfers between devices, to_everyone(): return lax.all_to_all(copies, axis, split_axis=0, concat_axis=0, tiled=True)  16.6 us
    ppermute x4, starting transfers between devices, from_behind(): return lax.ppermute(value, axis, pairs)  14.2 us
    pallas_call x1, Pallas kernels, body(): pl.pallas_call(table_kernel, out_shape=pltpu.VMEM((fields * SHARE_ROWS, L...  11.4 us
    ppermute x4, waiting for transfers between devices, from_behind(): return lax.ppermute(value, axis, pairs)  3.59 us
  transfers between devices with their start and end apart: 5, of which 2 were waited for; matrix products, arithmetic and copies ran while one was open for 0% of the time, Pallas kernels for 0%

profile of v1, /device:TPU:1, one launch (start us, length us, event | category | flops | bytes accessed | tf_op | source)
XLA Modules:
  0.0 82.5 jit_solution(15133692441925460357)
XLA Ops:
  0.0 0.0 copy-start
  0.0 0.8 %copy-done = f32[32,512]{1,0:T(8,128)S(1)} copy-done((f32[32,512]{1,0:T(8,128)S(1)}, f32[32,512]{1,0:T(8,128)}, u32[]{:S(2)}) %copy-start) | copy-done | bytes 65560
  0.8 1.5 %spread.1 = f32[32,8,512]{2,1,0:T(8,128)} custom-call(s32[8]{0:T(128)} %ids_ref.3, f32[32,512]{1,0:T(8,128)S(1)} %copy-done), custom_call_target="tpu_custom_call" | custom-call | tf_op jit(solution)/shard_map/spread/pallas_call | solution.py:172
  2.4 16.6 %all-to-all-start = ((f32[32,8,512]{2,1,0:T(8,128)}), f32[32,8,512]{2,1,0:T(8,128)S(1)}, u32[]{:S(2)}, u32[]{:S(2)}) async-start(f32[32,8,512]{2,1,0:T(8,128)} %spread.1), calls=%async_computation | async-start | bytes 1048576 | tf_op jit(solution)/shard_map/all_to_all | solution.py:21
  19.0 3.1 %collective-permute-start = (f32[32,512]{1,0:T(8,128)S(1)}, f32[32,512]{1,0:T(8,128)S(1)}, u32[]{:S(2)}, u32[]{:S(2)}) collective-permute-start(f32[32,512]{1,0:T(8,128)S(1)} %copy-done), channel_id=1, source_target_pairs={{0,32},{32,64},{64,96},{96,128},{128,160},{160,192},{192,224},{224... | collective-permute-start | bytes 196616 | tf_op jit(solution)/shard_map/ppermute | solution.py:17
  22.2 4.0 %collective-permute-start.1 = (f32[32,512]{1,0:T(8,128)S(1)}, f32[32,512]{1,0:T(8,128)S(1)}, u32[]{:S(2)}, u32[]{:S(2)}) collective-permute-start(f32[32,512]{1,0:T(8,128)S(1)} %copy-done), channel_id=1, source_target_pairs={{0,64},{32,96},{64,128},{96,160},{128,192},{160,224},{192,256},{22... | collective-permute-start | bytes 196616 | tf_op jit(solution)/shard_map/ppermute | solution.py:17
  26.2 4.0 %collective-permute-start.2 = (f32[32,512]{1,0:T(8,128)S(1)}, f32[32,512]{1,0:T(8,128)S(1)}, u32[]{:S(2)}, u32[]{:S(2)}) collective-permute-start(f32[32,512]{1,0:T(8,128)S(1)} %copy-done), channel_id=1, source_target_pairs={{0,96},{32,128},{64,160},{96,192},{128,224},{160,256},{192,288},{2... | collective-permute-start | bytes 196616 | tf_op jit(solution)/shard_map/ppermute | solution.py:17
  30.2 3.1 %collective-permute-start.3 = (f32[32,512]{1,0:T(8,128)S(1)}, f32[32,512]{1,0:T(8,128)S(1)}, u32[]{:S(2)}, u32[]{:S(2)}) collective-permute-start(f32[32,512]{1,0:T(8,128)S(1)} %copy-done), channel_id=1, source_target_pairs={{0,128},{32,160},{64,192},{96,224},{128,256},{160,288},{192,320},{... | collective-permute-start | bytes 196616 | tf_op jit(solution)/shard_map/ppermute | solution.py:17
  33.3 3.0 %collective-permute-done.refs_0_ = f32[32,512]{1,0:T(8,128)S(1)} collective-permute-done((f32[32,512]{1,0:T(8,128)S(1)}, f32[32,512]{1,0:T(8,128)S(1)}, u32[]{:S(2)}, u32[]{:S(2)}) %collective-permute-start) | collective-permute-done | bytes 65568 | tf_op jit(solution)/shard_map/ppermute | solution.py:17
  36.2 0.0 collective-permute-done.1.refs_1_
  36.2 0.0 collective-permute-done.2.refs_2_
  36.2 0.6 collective-permute-done.3.refs_3_
  36.8 0.0 all-to-all-done.arrived_ref
  36.9 11.4 %table.1 = f32[288,128]{1,0:T(8,128)S(1)} custom-call(s32[8]{0:T(128)} %ids_ref.3, f32[32,512]{1,0:T(8,128)S(1)} %copy-done, f32[32,8,512]{2,1,0:T(8,128)S(1)} %all-to-all-done.arrived_ref, f32[32,512]{1,0:T(8,128)S(1)} %collective-permute-done.refs_0_, f32[32,512]{1,0:T(8,128)S(1)} %collective-permute-done.1.refs_1_, ...), custom_call_target="tpu_custom_call" | custom-call | tf_op jit(solution)/shard_map/table/pallas_call | solution.py:182
  48.3 33.4 %all_to_all.10 = f32[32,1,1152]{2,1,0:T(1,128)S(1)} all-to-all(f32[32,1,1152]{2,1,0:T(1,128)S(1)} %bitcast.3), channel_id=1, replica_groups=mesh['wide'=32,'fields'=32] {'fields'}, dimensions={0} | all-to-all | bytes 294912 | tf_op jit(solution)/shard_map/all_to_all | solution.py:21
  81.7 0.9 %quotient.1 = f32[4,8,32]{2,1,0:T(8,128)} custom-call(f32[288,128]{1,0:T(8,128)S(1)} %bitcast.4), custom_call_target="tpu_custom_call" | custom-call | tf_op jit(solution)/shard_map/quotient/pallas_call | solution.py:194
Async XLA Ops:
  0.0 0.8 %copy-start = (f32[32,512]{1,0:T(8,128)S(1)}, f32[32,512]{1,0:T(8,128)}, u32[]{:S(2)}) copy-start(f32[32,512]{1,0:T(8,128)} %own_ref.1) | copy-start | bytes 196612
  2.4 34.5 %all-to-all-start = ((f32[32,8,512]{2,1,0:T(8,128)}), f32[32,8,512]{2,1,0:T(8,128)S(1)}, u32[]{:S(2)}, u32[]{:S(2)}) async-start(f32[32,8,512]{2,1,0:T(8,128)} %spread.1), calls=%async_computation | async-start | bytes 1048576 | tf_op jit(solution)/shard_map/all_to_all | solution.py:21
  19.0 17.2 %collective-permute-start = (f32[32,512]{1,0:T(8,128)S(1)}, f32[32,512]{1,0:T(8,128)S(1)}, u32[]{:S(2)}, u32[]{:S(2)}) collective-permute-start(f32[32,512]{1,0:T(8,128)S(1)} %copy-done), channel_id=1, source_target_pairs={{0,32},{32,64},{64,96},{96,128},{128,160},{160,192},{192,224},{224... | collective-permute-start | bytes 196616 | tf_op jit(solution)/shard_map/ppermute | solution.py:17
  22.2 14.1 %collective-permute-start.1 = (f32[32,512]{1,0:T(8,128)S(1)}, f32[32,512]{1,0:T(8,128)S(1)}, u32[]{:S(2)}, u32[]{:S(2)}) collective-permute-start(f32[32,512]{1,0:T(8,128)S(1)} %copy-done), channel_id=1, source_target_pairs={{0,64},{32,96},{64,128},{96,160},{128,192},{160,224},{192,256},{22... | collective-permute-start | bytes 196616 | tf_op jit(solution)/shard_map/ppermute | solution.py:17
  26.2 10.1 %collective-permute-start.2 = (f32[32,512]{1,0:T(8,128)S(1)}, f32[32,512]{1,0:T(8,128)S(1)}, u32[]{:S(2)}, u32[]{:S(2)}) collective-permute-start(f32[32,512]{1,0:T(8,128)S(1)} %copy-done), channel_id=1, source_target_pairs={{0,96},{32,128},{64,160},{96,192},{128,224},{160,256},{192,288},{2... | collective-permute-start | bytes 196616 | tf_op jit(solution)/shard_map/ppermute | solution.py:17
  30.2 6.7 %collective-permute-start.3 = (f32[32,512]{1,0:T(8,128)S(1)}, f32[32,512]{1,0:T(8,128)S(1)}, u32[]{:S(2)}, u32[]{:S(2)}) collective-permute-start(f32[32,512]{1,0:T(8,128)S(1)} %copy-done), channel_id=1, source_target_pairs={{0,128},{32,160},{64,192},{96,224},{128,256},{160,288},{192,320},{... | collective-permute-start | bytes 196616 | tf_op jit(solution)/shard_map/ppermute | solution.py:17

commit v2 on v1

v2 whole, which is shorter than its diff:
```python
import jax
import jax.numpy as jnp
from jax import lax
from jax.experimental import pallas as pl
from jax.experimental.pallas import tpu as pltpu
from jax.sharding import PartitionSpec as P

STEPS = 4
UNROLL = 32
LANES = 128
SUBLANES = 8
SHARE_ROWS = SUBLANES + 1


def from_behind(value, axis, steps):
    count = lax.axis_size(axis)
    pairs = [(source, (source + steps) % count) for source in range(count)]
    return lax.ppermute(value, axis, pairs)


def to_everyone(copies, axis):
    return lax.all_to_all(copies, axis, split_axis=0, concat_axis=0, tiled=True)


def spread_kernel(ids_ref, vectors_ref, copies_ref, rows_ref):
    row_count = vectors_ref.shape[0]
    for q in range(rows_ref.shape[0]):
        rows_ref[q : q + 1, :] = vectors_ref[pl.ds(lax.rem(ids_ref[q], row_count), 1), :]
    rows = rows_ref[...]
    for peer in range(copies_ref.shape[0]):
        copies_ref[peer] = rows


def lane_at(offset):
    lane = lax.broadcasted_iota(jnp.int32, (SUBLANES, LANES), 1)
    sublane = lax.broadcasted_iota(jnp.int32, (SUBLANES, LANES), 0)
    return lane == sublane + offset


def column_sum(tiles):
    folded = tiles[0]
    for tile in tiles[1:]:
        folded = folded + tile
    return jnp.sum(folded, axis=1, keepdims=True)


def by_group(columns):
    lane = lax.broadcasted_iota(jnp.int32, (SUBLANES, LANES), 1)
    size = LANES // len(columns)
    tile = jnp.broadcast_to(columns[-1], (SUBLANES, LANES))
    for g in range(len(columns) - 2, -1, -1):
        tile = jnp.where(lane < (g + 1) * size, columns[g], tile)
    return tile


def every_row(ref, row):
    return jnp.broadcast_to(ref[pl.ds(row, 1), :], (SUBLANES, LANES))


def turn_kernel(own_ref, turned_ref):
    row_count, width = own_ref.shape
    for t in range(width // LANES):
        at = slice(t * LANES, (t + 1) * LANES)
        for a in range(SUBLANES):
            rows = jnp.concatenate(
                [
                    jnp.broadcast_to(own_ref[v : v + 1, at], (row_count, LANES))
                    for v in range(a, row_count, SUBLANES)
                ],
                axis=0,
            )
            turned_ref[pl.ds(t * LANES * SUBLANES + a, LANES, stride=SUBLANES), :] = rows.T


def table_kernel(ids_ref, own_ref, turned_ref, arrived_ref, *refs):
    partner_refs = refs[:STEPS]
    out_ref, pivots_ref, fields_ref, splat_ref = refs[STEPS:]
    row_count, width = own_ref.shape
    pivot_count = pivots_ref.shape[0]
    tiles = width // LANES
    groups = row_count // SUBLANES
    for q in range(pivot_count):
        pivots_ref[q : q + 1, :] = arrived_ref[lax.div(ids_ref[q], row_count), q : q + 1, :]

    for t in range(tiles):
        at = slice(t * LANES, (t + 1) * LANES)
        for cg in range(groups):
            rows = [ref[cg * SUBLANES : (cg + 1) * SUBLANES, at] for ref in partner_refs]
            fields_ref[cg * width + t * LANES : cg * width + (t + 1) * LANES, :] = jnp.concatenate(
                rows * groups, axis=0
            ).T
        for q in range(pivot_count):
            splat_ref[q * width + t * LANES : q * width + (t + 1) * LANES, :] = jnp.broadcast_to(
                pivots_ref[q : q + 1, at], (LANES, LANES)
            ).T

    def some_fields(step, sums):
        sums = list(sums)
        for i in range(UNROLL):
            f = step * UNROLL + i
            own = turned_ref[pl.ds(f * SUBLANES, SUBLANES), :]
            partners = [every_row(fields_ref, cg * width + f) for cg in range(groups)]
            for q in range(pivot_count):
                larger = jnp.maximum(own, every_row(splat_ref, q * width + f))
                for cg in range(groups):
                    k = q * groups + cg
                    sums[k] = sums[k] + jnp.minimum(larger, partners[cg])
        return tuple(sums)

    first = []
    for q in range(pivot_count):
        smaller = by_group(
            [
                column_sum(
                    [
                        jnp.minimum(
                            own_ref[g * SUBLANES : (g + 1) * SUBLANES, t * LANES : (t + 1) * LANES],
                            pivots_ref[q : q + 1, t * LANES : (t + 1) * LANES],
                        )
                        for t in range(tiles)
                    ]
                )
                for g in range(groups)
            ]
        )
        first.extend([smaller] * groups)
    sums = lax.fori_loop(0, width // UNROLL, some_fields, tuple(first))

    def totals(ref, g):
        rows = slice(g * SUBLANES, (g + 1) * SUBLANES)
        return column_sum([ref[rows, t * LANES : (t + 1) * LANES] for t in range(tiles)])

    own_row = jnp.zeros((SUBLANES, LANES), jnp.float32)
    for g in range(groups):
        own_row = own_row + jnp.where(lane_at(row_count + g * SUBLANES), totals(own_ref, g), 0.0)
    own_row = jnp.sum(own_row, axis=0, keepdims=True) + totals(pivots_ref, 0)
    lane = lax.broadcasted_iota(jnp.int32, (SUBLANES, LANES), 1)
    for cg in range(groups):
        partner_row = jnp.sum(fields_ref[cg * width : (cg + 1) * width, :], axis=0, keepdims=True)
        rows = jnp.where(lane < STEPS * SUBLANES, partner_row, own_row)
        for q in range(pivot_count):
            at = (q * groups + cg) * SHARE_ROWS
            out_ref[at : at + SUBLANES, :] = sums[q * groups + cg]
            out_ref[at + SUBLANES : at + SUBLANES + 1, :] = rows[q : q + 1, :]


def quotient_kernel(arrived_ref, out_ref):
    steps, _, row_count = out_ref.shape
    peers = arrived_ref.shape[0] // SHARE_ROWS
    groups = row_count // SUBLANES
    size = LANES // groups
    numerator = arrived_ref[0:SUBLANES, :]
    total = arrived_ref[SUBLANES : SUBLANES + 1, :]
    for peer in range(1, peers):
        at = peer * SHARE_ROWS
        numerator = numerator + arrived_ref[at : at + SUBLANES, :]
        total = total + arrived_ref[at + SUBLANES : at + SUBLANES + 1, :]
    totals = jnp.broadcast_to(total, (SUBLANES, LANES))
    own = by_group(
        [
            jnp.sum(jnp.where(lane_at(size + g * SUBLANES), totals, 0.0), axis=1, keepdims=True)
            for g in range(groups)
        ]
    )
    partner = jnp.concatenate([totals[:, :size]] * groups, axis=1)
    turned = (1.5 * numerator / (own + partner)).T
    for s in range(steps):
        rows = [g * size + s * SUBLANES for g in range(groups)]
        out_ref[s] = jnp.concatenate([turned[r : r + SUBLANES, :] for r in rows], axis=1)


def in_vmem(array):
    return pltpu.with_memory_space_constraint(array, pltpu.VMEM)


def body(vectors, pivot_ids):
    row_count, width = vectors.shape
    pivot_count = pivot_ids.shape[0]
    wide = lax.axis_size("wide")
    fields = lax.axis_size("fields")
    smem = pl.BlockSpec(memory_space=pltpu.SMEM)
    vmem = pl.BlockSpec(memory_space=pltpu.VMEM)
    copies = pl.pallas_call(
        spread_kernel,
        out_shape=pltpu.VMEM((wide, pivot_count, width), jnp.float32),
        in_specs=[smem, vmem],
        out_specs=vmem,
        scratch_shapes=[pltpu.VMEM((pivot_count, width), jnp.float32)],
        name="spread",
    )(pivot_ids, in_vmem(vectors))
    arrived = to_everyone(copies, "wide")
    partners = [from_behind(vectors, "wide", s) for s in range(1, STEPS + 1)]
    turned = pl.pallas_call(
        turn_kernel,
        out_shape=pltpu.VMEM((width * SUBLANES, LANES), jnp.float32),
        in_specs=[vmem],
        out_specs=vmem,
        name="turn",
    )(in_vmem(vectors))
    table = pl.pallas_call(
        table_kernel,
        out_shape=pltpu.VMEM((fields * SHARE_ROWS, LANES), jnp.float32),
        in_specs=[smem] + [vmem] * (3 + STEPS),
        out_specs=vmem,
        scratch_shapes=[
            pltpu.VMEM((pivot_count, width), jnp.float32),
            pltpu.VMEM((row_count // SUBLANES * width, LANES), jnp.float32),
            pltpu.VMEM((pivot_count * width, LANES), jnp.float32),
        ],
        name="table",
    )(pivot_ids, *(in_vmem(a) for a in (vectors, turned, arrived, *partners)))
    shares = to_everyone(table.reshape(fields, 1, SHARE_ROWS * LANES), "fields")
    quotient = pl.pallas_call(
        quotient_kernel,
        out_shape=jax.ShapeDtypeStruct((STEPS, SUBLANES, row_count), jnp.float32),
        in_specs=[vmem],
        out_specs=vmem,
        name="quotient",
    )(in_vmem(shares.reshape(fields * SHARE_ROWS, LANES)))
    return jnp.transpose(quotient, (2, 0, 1))


def solution(mesh):
    placed = (P("wide", "fields"), P())
    return jax.shard_map(
        body, mesh=mesh, in_specs=placed, out_specs=P("wide", None, "fields"), check_vma=False
    )
```

time: 82.9 us -> 79.7 us (0.961)
  Pallas kernels: 13.8 us -> 9.78 us
  waiting for transfers between devices: 3.59 us -> 6.85 us
  blocking collectives: 33.4 us -> 31.8 us
  starting transfers between devices: 30.9 us -> 30 us
    pallas_call x1, Pallas kernels: 11.4 us -> 6.74 us  [body(): pl.pallas_call(table_kernel, out_shape=pltpu.VMEM((fields * SHARE_ROWS, L...]
    ppermute x4, waiting for transfers between devices: 3.59 us -> 6.84 us  [from_behind(): return lax.ppermute(value, axis, pairs)]
    all_to_all x1, blocking collectives: 33.4 us -> 31.8 us  [to_everyone(): return lax.all_to_all(copies, axis, split_axis=0, concat_axis=0, tiled=True)]
    ppermute x4, starting transfers between devices: 14.2 us -> 13.3 us  [from_behind(): return lax.ppermute(value, axis, pairs)]
  transfers between devices with their start and end apart: 5 -> 5, of which waited for: 2 -> 3; matrix products, arithmetic and copies ran while one was open for 0% -> 0% of each run, Pallas kernels for 0% -> 1%
where the time goes in v2:
time: 79.7 us; the launch traced here: 79.3 us
  blocking collectives  31.8 us (40%)
  starting transfers between devices  30 us (38%)
  Pallas kernels  9.78 us (12%)
  waiting for transfers between devices  6.85 us (9%)
  local copies, waits for them, and re-layouts  0.84 us (1%)
    all_to_all x1, blocking collectives, to_everyone(): return lax.all_to_all(copies, axis, split_axis=0, concat_axis=0, tiled=True)  31.8 us
    all_to_all x1, starting transfers between devices, to_everyone(): return lax.all_to_all(copies, axis, split_axis=0, concat_axis=0, tiled=True)  16.6 us
    ppermute x4, starting transfers between devices, from_behind(): return lax.ppermute(value, axis, pairs)  13.3 us
    ppermute x4, waiting for transfers between devices, from_behind(): return lax.ppermute(value, axis, pairs)  6.84 us
    pallas_call x1, Pallas kernels, body(): pl.pallas_call(table_kernel, out_shape=pltpu.VMEM((fields * SHARE_ROWS, L...  6.74 us
  transfers between devices with their start and end apart: 5, of which 3 were waited for; matrix products, arithmetic and copies ran while one was open for 0% of the time, Pallas kernels for 1%

profile of v2, /device:TPU:1, one launch (start us, length us, event | category | flops | bytes accessed | tf_op | source)
XLA Modules:
  0.0 79.3 jit_solution(11669824784813885449)
XLA Ops:
  0.0 0.0 copy-start
  0.0 0.8 %copy-done = f32[32,512]{1,0:T(8,128)S(1)} copy-done((f32[32,512]{1,0:T(8,128)S(1)}, f32[32,512]{1,0:T(8,128)}, u32[]{:S(2)}) %copy-start) | copy-done | bytes 65560
  0.8 1.5 %spread.1 = f32[32,8,512]{2,1,0:T(8,128)} custom-call(s32[8]{0:T(128)} %ids_ref.3, f32[32,512]{1,0:T(8,128)S(1)} %copy-done), custom_call_target="tpu_custom_call" | custom-call | tf_op jit(solution)/shard_map/spread/pallas_call | solution.py:183
  2.4 16.6 %all-to-all-start = ((f32[32,8,512]{2,1,0:T(8,128)}), f32[32,8,512]{2,1,0:T(8,128)S(1)}, u32[]{:S(2)}, u32[]{:S(2)}) async-start(f32[32,8,512]{2,1,0:T(8,128)} %spread.1), calls=%async_computation | async-start | bytes 1048576 | tf_op jit(solution)/shard_map/all_to_all | solution.py:22
  19.0 4.9 %collective-permute-start.2 = (f32[32,512]{1,0:T(8,128)S(1)}, f32[32,512]{1,0:T(8,128)S(1)}, u32[]{:S(2)}, u32[]{:S(2)}) collective-permute-start(f32[32,512]{1,0:T(8,128)S(1)} %copy-done), channel_id=1, source_target_pairs={{0,96},{32,128},{64,160},{96,192},{128,224},{160,256},{192,288},{2... | collective-permute-start | bytes 196616 | tf_op jit(solution)/shard_map/ppermute | solution.py:18
  24.0 2.2 %collective-permute-start.1 = (f32[32,512]{1,0:T(8,128)S(1)}, f32[32,512]{1,0:T(8,128)S(1)}, u32[]{:S(2)}, u32[]{:S(2)}) collective-permute-start(f32[32,512]{1,0:T(8,128)S(1)} %copy-done), channel_id=1, source_target_pairs={{0,64},{32,96},{64,128},{96,160},{128,192},{160,224},{192,256},{22... | collective-permute-start | bytes 196616 | tf_op jit(solution)/shard_map/ppermute | solution.py:18
  26.2 3.1 %collective-permute-start = (f32[32,512]{1,0:T(8,128)S(1)}, f32[32,512]{1,0:T(8,128)S(1)}, u32[]{:S(2)}, u32[]{:S(2)}) collective-permute-start(f32[32,512]{1,0:T(8,128)S(1)} %copy-done), channel_id=1, source_target_pairs={{0,32},{32,64},{64,96},{96,128},{128,160},{160,192},{192,224},{224... | collective-permute-start | bytes 196616 | tf_op jit(solution)/shard_map/ppermute | solution.py:18
  29.3 3.1 %collective-permute-start.3 = (f32[32,512]{1,0:T(8,128)S(1)}, f32[32,512]{1,0:T(8,128)S(1)}, u32[]{:S(2)}, u32[]{:S(2)}) collective-permute-start(f32[32,512]{1,0:T(8,128)S(1)} %copy-done), channel_id=1, source_target_pairs={{0,128},{32,160},{64,192},{96,224},{128,256},{160,288},{192,320},{... | collective-permute-start | bytes 196616 | tf_op jit(solution)/shard_map/ppermute | solution.py:18
  32.4 0.6 turn.1.turned_ref
  33.0 0.6 collective-permute-done.2.refs_2_
  33.6 3.9 %collective-permute-done.1.refs_1_ = f32[32,512]{1,0:T(8,128)S(1)} collective-permute-done((f32[32,512]{1,0:T(8,128)S(1)}, f32[32,512]{1,0:T(8,128)S(1)}, u32[]{:S(2)}, u32[]{:S(2)}) %collective-permute-start.1) | collective-permute-done | bytes 65568 | tf_op jit(solution)/shard_map/ppermute | solution.py:18
  37.5 2.3 %collective-permute-done.refs_0_ = f32[32,512]{1,0:T(8,128)S(1)} collective-permute-done((f32[32,512]{1,0:T(8,128)S(1)}, f32[32,512]{1,0:T(8,128)S(1)}, u32[]{:S(2)}, u32[]{:S(2)}) %collective-permute-start) | collective-permute-done | bytes 65568 | tf_op jit(solution)/shard_map/ppermute | solution.py:18
  39.8 0.0 collective-permute-done.3.refs_3_
  39.8 0.0 all-to-all-done.arrived_ref
  39.8 6.7 %table.1 = f32[288,128]{1,0:T(8,128)S(1)} custom-call(s32[8]{0:T(128)} %ids_ref.3, f32[32,512]{1,0:T(8,128)S(1)} %copy-done, f32[4096,128]{1,0:T(8,128)S(1)} %turn.1.turned_ref, f32[32,8,512]{2,1,0:T(8,128)S(1)} %all-to-all-done.arrived_ref, f32[32,512]{1,0:T(8,128)S(1)} %collective-permute-done.refs_0_, f32[32,512]{1,0:T(8,128)S(1)} %collective-permute-done.1.refs_1_, ...), custom_call_target="tpu_custom_call" | custom-call | tf_op jit(solution)/shard_map/table/pallas_call | solution.py:200
  46.6 31.8 %all_to_all.10 = f32[32,1,1152]{2,1,0:T(1,128)S(1)} all-to-all(f32[32,1,1152]{2,1,0:T(1,128)S(1)} %bitcast.3), channel_id=1, replica_groups=mesh['wide'=32,'fields'=32] {'fields'}, dimensions={0} | all-to-all | bytes 294912 | tf_op jit(solution)/shard_map/all_to_all | solution.py:22
  78.4 0.9 %quotient.1 = f32[4,8,32]{2,1,0:T(8,128)} custom-call(f32[288,128]{1,0:T(8,128)S(1)} %bitcast.4), custom_call_target="tpu_custom_call" | custom-call | tf_op jit(solution)/shard_map/quotient/pallas_call | solution.py:213
Async XLA Ops:
  0.0 0.8 %copy-start = (f32[32,512]{1,0:T(8,128)S(1)}, f32[32,512]{1,0:T(8,128)}, u32[]{:S(2)}) copy-start(f32[32,512]{1,0:T(8,128)} %own_ref.3) | copy-start | bytes 196612
  2.4 37.4 %all-to-all-start = ((f32[32,8,512]{2,1,0:T(8,128)}), f32[32,8,512]{2,1,0:T(8,128)S(1)}, u32[]{:S(2)}, u32[]{:S(2)}) async-start(f32[32,8,512]{2,1,0:T(8,128)} %spread.1), calls=%async_computation | async-start | bytes 1048576 | tf_op jit(solution)/shard_map/all_to_all | solution.py:22
  19.0 14.6 %collective-permute-start.2 = (f32[32,512]{1,0:T(8,128)S(1)}, f32[32,512]{1,0:T(8,128)S(1)}, u32[]{:S(2)}, u32[]{:S(2)}) collective-permute-start(f32[32,512]{1,0:T(8,128)S(1)} %copy-done), channel_id=1, source_target_pairs={{0,96},{32,128},{64,160},{96,192},{128,224},{160,256},{192,288},{2... | collective-permute-start | bytes 196616 | tf_op jit(solution)/shard_map/ppermute | solution.py:18
  24.0 13.5 %collective-permute-start.1 = (f32[32,512]{1,0:T(8,128)S(1)}, f32[32,512]{1,0:T(8,128)S(1)}, u32[]{:S(2)}, u32[]{:S(2)}) collective-permute-start(f32[32,512]{1,0:T(8,128)S(1)} %copy-done), channel_id=1, source_target_pairs={{0,64},{32,96},{64,128},{96,160},{128,192},{160,224},{192,256},{22... | collective-permute-start | bytes 196616 | tf_op jit(solution)/shard_map/ppermute | solution.py:18
  26.2 13.7 %collective-permute-start = (f32[32,512]{1,0:T(8,128)S(1)}, f32[32,512]{1,0:T(8,128)S(1)}, u32[]{:S(2)}, u32[]{:S(2)}) collective-permute-start(f32[32,512]{1,0:T(8,128)S(1)} %copy-done), channel_id=1, source_target_pairs={{0,32},{32,64},{64,96},{96,128},{128,160},{160,192},{192,224},{224... | collective-permute-start | bytes 196616 | tf_op jit(solution)/shard_map/ppermute | solution.py:18
  29.3 10.6 %collective-permute-start.3 = (f32[32,512]{1,0:T(8,128)S(1)}, f32[32,512]{1,0:T(8,128)S(1)}, u32[]{:S(2)}, u32[]{:S(2)}) collective-permute-start(f32[32,512]{1,0:T(8,128)S(1)} %copy-done), channel_id=1, source_target_pairs={{0,128},{32,160},{64,192},{96,224},{128,256},{160,288},{192,320},{... | collective-permute-start | bytes 196616 | tf_op jit(solution)/shard_map/ppermute | solution.py:18

commit v3 on v2

v3 whole, which is shorter than its diff:
```python
import jax
import jax.numpy as jnp
from jax import lax
from jax.experimental import pallas as pl
from jax.experimental.pallas import tpu as pltpu
from jax.sharding import PartitionSpec as P


STEPS = 4
UNROLL = 32
HALVES = 2
LANES = 128
SUBLANES = 8
SHARE_ROWS = SUBLANES + 2


def from_behind(value, axis, steps):
    count = lax.axis_size(axis)
    pairs = [(source, (source + steps) % count) for source in range(count)]
    return lax.ppermute(value, axis, pairs)


def to_everyone(copies, axis):
    return lax.all_to_all(copies, axis, split_axis=0, concat_axis=0, tiled=True)


def spread_kernel(ids_ref, vectors_ref, copies_ref, own_ref, rows_ref):
    row_count = vectors_ref.shape[0]
    for q in range(rows_ref.shape[0]):
        rows_ref[q : q + 1, :] = vectors_ref[pl.ds(lax.rem(ids_ref[q], row_count), 1), :]
    rows = rows_ref[...]
    for peer in range(copies_ref.shape[0]):
        copies_ref[peer] = rows
    own_ref[...] = vectors_ref[...]


def lane_at(offset):
    lane = lax.broadcasted_iota(jnp.int32, (SUBLANES, LANES), 1)
    sublane = lax.broadcasted_iota(jnp.int32, (SUBLANES, LANES), 0)
    return lane == sublane + offset


def column_sum(tiles):
    folded = tiles[0]
    for tile in tiles[1:]:
        folded = folded + tile
    return jnp.sum(folded, axis=1, keepdims=True)


def by_group(columns):
    lane = lax.broadcasted_iota(jnp.int32, (SUBLANES, LANES), 1)
    size = LANES // len(columns)
    tile = jnp.broadcast_to(columns[-1], (SUBLANES, LANES))
    for g in range(len(columns) - 2, -1, -1):
        tile = jnp.where(lane < (g + 1) * size, columns[g], tile)
    return tile


def every_row(ref, row):
    return jnp.broadcast_to(ref[pl.ds(row, 1), :], (SUBLANES, LANES))


def turn_kernel(own_ref, turned_ref):
    row_count, width = own_ref.shape
    copies = LANES // HALVES * SUBLANES // row_count
    for t in range(width // LANES):
        at = slice(t * LANES, (t + 1) * LANES)
        for a in range(SUBLANES):
            rows = [
                jnp.broadcast_to(own_ref[v : v + 1, at], (copies, LANES))
                for v in range(a, row_count, SUBLANES)
            ]
            turned_ref[pl.ds(t * LANES * SUBLANES + a, LANES, stride=SUBLANES), :] = jnp.concatenate(
                rows * HALVES, axis=0
            ).T


def turn_partners(partner_refs, fields_ref):
    row_count, width = partner_refs[0].shape
    groups = row_count // SUBLANES
    for cp in range(groups // HALVES):
        for t in range(width // LANES):
            at = slice(t * LANES, (t + 1) * LANES)
            rows = []
            for h in range(HALVES):
                first = (cp * HALVES + h) * SUBLANES
                rows.extend([ref[first : first + SUBLANES, at] for ref in partner_refs] * groups)
            fields_ref[cp * width + t * LANES : cp * width + (t + 1) * LANES, :] = jnp.concatenate(
                rows, axis=0
            ).T


def sum_fields(turned_ref, splat_ref, fields_ref, smaller):
    width = turned_ref.shape[0] // SUBLANES
    pairs = fields_ref.shape[0] // width
    pivot_count = len(smaller)

    def some_fields(step, sums):
        sums = list(sums)
        for i in range(UNROLL):
            f = step * UNROLL + i
            own = turned_ref[pl.ds(f * SUBLANES, SUBLANES), :]
            partners = [every_row(fields_ref, cp * width + f) for cp in range(pairs)]
            for q in range(pivot_count):
                larger = jnp.maximum(own, every_row(splat_ref, q * width + f))
                for cp in range(pairs):
                    k = q * pairs + cp
                    sums[k] = sums[k] + jnp.minimum(larger, partners[cp])
        return tuple(sums)

    first = tuple(tile for tile in smaller for _ in range(pairs))
    return lax.fori_loop(0, width // UNROLL, some_fields, first)


def partner_totals(fields_ref, width):
    return [
        jnp.sum(fields_ref[first : first + width, :], axis=0, keepdims=True)
        for first in range(0, fields_ref.shape[0], width)
    ]


def early_kernel(ids_ref, own_ref, turned_ref, arrived_ref, *refs):
    count = STEPS // HALVES
    partner_refs = refs[:count]
    splat_ref, smaller_ref, totals_ref, sums_ref, partners_ref, pivots_ref, fields_ref = refs[count:]
    row_count, width = own_ref.shape
    pivot_count = pivots_ref.shape[0]
    tiles = width // LANES
    groups = row_count // SUBLANES
    for q in range(pivot_count):
        pivots_ref[q : q + 1, :] = arrived_ref[lax.div(ids_ref[q], row_count), q : q + 1, :]
    turn_partners(partner_refs, fields_ref)
    for t in range(tiles):
        for q in range(pivot_count):
            splat_ref[q * width + t * LANES : q * width + (t + 1) * LANES, :] = jnp.broadcast_to(
                pivots_ref[q : q + 1, t * LANES : (t + 1) * LANES], (LANES, LANES)
            ).T
    smaller = []
    for q in range(pivot_count):
        columns = [
            column_sum(
                [
                    jnp.minimum(
                        own_ref[g * SUBLANES : (g + 1) * SUBLANES, t * LANES : (t + 1) * LANES],
                        pivots_ref[q : q + 1, t * LANES : (t + 1) * LANES],
                    )
                    for t in range(tiles)
                ]
            )
            for g in range(groups)
        ]
        smaller.append(by_group(columns * HALVES))
        smaller_ref[q * SUBLANES : (q + 1) * SUBLANES, :] = smaller[-1]
    sums = sum_fields(turned_ref, splat_ref, fields_ref, smaller)
    for k, tile in enumerate(sums):
        sums_ref[k * SUBLANES : (k + 1) * SUBLANES, :] = tile

    def totals(ref, g):
        rows = slice(g * SUBLANES, (g + 1) * SUBLANES)
        return column_sum([ref[rows, t * LANES : (t + 1) * LANES] for t in range(tiles)])

    own_row = jnp.zeros((SUBLANES, LANES), jnp.float32)
    for g in range(groups):
        own_row = own_row + jnp.where(lane_at(g * SUBLANES), totals(own_ref, g), 0.0)
    totals_ref[...] = jnp.sum(own_row, axis=0, keepdims=True) + totals(pivots_ref, 0)
    for cp, row in enumerate(partner_totals(fields_ref, width)):
        partners_ref[cp * SUBLANES : (cp + 1) * SUBLANES, :] = jnp.broadcast_to(row, (SUBLANES, LANES))


def late_kernel(turned_ref, splat_ref, smaller_ref, totals_ref, sums_ref, partners_ref, *refs):
    count = STEPS // HALVES
    partner_refs = refs[:count]
    out_ref, fields_ref = refs[count:]
    row_count, width = partner_refs[0].shape
    groups = row_count // SUBLANES
    pairs = groups // HALVES
    pivot_count = smaller_ref.shape[0] // SUBLANES
    turn_partners(partner_refs, fields_ref)
    smaller = [smaller_ref[q * SUBLANES : (q + 1) * SUBLANES, :] for q in range(pivot_count)]
    sums = sum_fields(turned_ref, splat_ref, fields_ref, smaller)

    lane = lax.broadcasted_iota(jnp.int32, (SUBLANES, LANES), 1)
    half = LANES // HALVES

    def joined(early, late):
        return (
            jnp.where(lane < half, early, pltpu.roll(late, half, 1)),
            jnp.where(lane < half, pltpu.roll(early, half, 1), late),
        )

    partners = [
        joined(
            partners_ref[cp * SUBLANES : (cp + 1) * SUBLANES, :],
            jnp.broadcast_to(row, (SUBLANES, LANES)),
        )
        for cp, row in enumerate(partner_totals(fields_ref, width))
    ]
    for q in range(pivot_count):
        for cp in range(pairs):
            k = q * pairs + cp
            tiles = joined(sums_ref[k * SUBLANES : (k + 1) * SUBLANES, :], sums[k])
            for h in range(HALVES):
                at = (k * HALVES + h) * SHARE_ROWS
                out_ref[at : at + SUBLANES, :] = tiles[h]
                out_ref[at + SUBLANES : at + SUBLANES + 1, :] = partners[cp][h][:1, :]
                out_ref[at + SUBLANES + 1 : at + SUBLANES + 2, :] = totals_ref[q : q + 1, :]


def quotient_kernel(arrived_ref, out_ref):
    steps, _, row_count = out_ref.shape
    peers = arrived_ref.shape[0] // SHARE_ROWS
    groups = row_count // SUBLANES
    count = steps // HALVES
    share = arrived_ref[0:SUBLANES, :], arrived_ref[SUBLANES:SHARE_ROWS, :]
    for peer in range(1, peers):
        at = peer * SHARE_ROWS
        share = (
            share[0] + arrived_ref[at : at + SUBLANES, :],
            share[1] + arrived_ref[at + SUBLANES : at + SHARE_ROWS, :],
        )
    numerator, totals = share
    row = jnp.broadcast_to(totals[1:2, :], (SUBLANES, LANES))
    columns = [
        jnp.sum(jnp.where(lane_at(g * SUBLANES), row, 0.0), axis=1, keepdims=True) for g in range(groups)
    ]
    turned = (1.5 * numerator / (by_group(columns * HALVES) + totals[0:1, :])).T
    for s in range(steps):
        k, i = divmod(s, count)
        rows = [(k * groups + g) * count * SUBLANES + i * SUBLANES for g in range(groups)]
        out_ref[s] = jnp.concatenate([turned[r : r + SUBLANES, :] for r in rows], axis=1)


def in_vmem(array):
    return pltpu.with_memory_space_constraint(array, pltpu.VMEM)


def body(vectors, pivot_ids):
    row_count, width = vectors.shape
    pivot_count = pivot_ids.shape[0]
    wide = lax.axis_size("wide")
    fields = lax.axis_size("fields")
    pairs = row_count // SUBLANES // HALVES
    count = STEPS // HALVES
    smem = pl.BlockSpec(memory_space=pltpu.SMEM)
    vmem = pl.BlockSpec(memory_space=pltpu.VMEM)
    small = pltpu.CompilerParams(vmem_limit_bytes=16 << 20)
    copies, vectors = pl.pallas_call(
        spread_kernel,
        out_shape=[
            jax.ShapeDtypeStruct((wide, pivot_count, width), jnp.float32),
            pltpu.VMEM(vectors.shape, jnp.float32),
        ],
        in_specs=[smem, vmem],
        out_specs=[vmem, vmem],
        scratch_shapes=[pltpu.VMEM((pivot_count, width), jnp.float32)],
        name="spread",
    )(pivot_ids, vectors)
    arrived = to_everyone(copies, "wide")
    partners = []
    for s in range(1, STEPS + 1):
        partners.append(in_vmem(from_behind(vectors, "wide", s)))
    turned = pl.pallas_call(
        turn_kernel,
        out_shape=pltpu.VMEM((width * SUBLANES, LANES), jnp.float32),
        in_specs=[vmem],
        out_specs=vmem,
        compiler_params=small,
        name="turn",
    )(in_vmem(vectors))
    between = pl.pallas_call(
        early_kernel,
        out_shape=[
            pltpu.VMEM((pivot_count * width, LANES), jnp.float32),
            pltpu.VMEM((pivot_count * SUBLANES, LANES), jnp.float32),
            pltpu.VMEM((pivot_count, LANES), jnp.float32),
            pltpu.VMEM((pivot_count * pairs * SUBLANES, LANES), jnp.float32),
            pltpu.VMEM((pairs * SUBLANES, LANES), jnp.float32),
        ],
        in_specs=[smem] + [vmem] * (3 + count),
        out_specs=[vmem] * 5,
        scratch_shapes=[
            pltpu.VMEM((pivot_count, width), jnp.float32),
            pltpu.VMEM((pairs * width, LANES), jnp.float32),
        ],
        compiler_params=small,
        name="early",
    )(pivot_ids, in_vmem(vectors), in_vmem(turned), in_vmem(arrived), *partners[:count])
    table = pl.pallas_call(
        late_kernel,
        out_shape=pltpu.VMEM((fields * SHARE_ROWS, LANES), jnp.float32),
        in_specs=[vmem] * (6 + count),
        out_specs=vmem,
        scratch_shapes=[pltpu.VMEM((pairs * width, LANES), jnp.float32)],
        compiler_params=small,
        name="late",
    )(in_vmem(turned), *(in_vmem(a) for a in between), *partners[count:])
    shares = to_everyone(table.reshape(fields, 1, SHARE_ROWS * LANES), "fields")
    quotient = pl.pallas_call(
        quotient_kernel,
        out_shape=jax.ShapeDtypeStruct((STEPS, SUBLANES, row_count), jnp.float32),
        in_specs=[vmem],
        out_specs=vmem,
        name="quotient",
    )(in_vmem(shares.reshape(fields * SHARE_ROWS, LANES)))
    return jnp.transpose(quotient, (2, 0, 1))


def solution(mesh):
    placed = (P("wide", "fields"), P())
    return jax.shard_map(
        body, mesh=mesh, in_specs=placed, out_specs=P("wide", None, "fields"), check_vma=False
    )
```

time: 79.7 us -> 78.7 us (0.987)
  waiting for transfers between devices: 6.85 us -> 2.37 us
  blocking collectives: 31.8 us -> 34.4 us
  local copies, waits for them, and re-layouts: 0.84 us -> 0.01 us
  Pallas kernels: 9.78 us -> 10.6 us
  starting transfers between devices: 30 us -> 30.8 us
    ppermute x4, waiting for transfers between devices: 6.84 us -> 2.37 us  [from_behind(): return lax.ppermute(value, axis, pairs)]
    all_to_all x1, blocking collectives: 31.8 us -> 34.4 us  [to_everyone(): return lax.all_to_all(copies, axis, split_axis=0, concat_axis=0, tiled=True)]
    ppermute x4, starting transfers between devices: 13.3 us -> 14.2 us  [from_behind(): return lax.ppermute(value, axis, pairs)]
    pallas_call x2 -> x3, Pallas kernels: 8.27 us -> 9.15 us  [the longest x1 4.23 us: body(): pl.pallas_call(early_kernel, out_shape=[pltpu.VMEM((pivot_count * width,...]
    unnamed x2, local copies, waits for them, and re-layouts: 0.84 us -> 0.01 us
  transfers between devices with their start and end apart: 5 -> 5, of which waited for: 3 -> 1; matrix products, arithmetic and copies ran while one was open for 0% -> 0% of each run, Pallas kernels for 1% -> 6%
where the time goes in v3:
time: 78.7 us; the launch traced here: 78.3 us
  blocking collectives  34.4 us (44%)
  starting transfers between devices  30.8 us (39%)
  Pallas kernels  10.6 us (13%)
  waiting for transfers between devices  2.37 us (3%)
    all_to_all x1, blocking collectives, to_everyone(): return lax.all_to_all(copies, axis, split_axis=0, concat_axis=0, tiled=True)  34.4 us
    all_to_all x1, starting transfers between devices, to_everyone(): return lax.all_to_all(copies, axis, split_axis=0, concat_axis=0, tiled=True)  16.6 us
    ppermute x4, starting transfers between devices, from_behind(): return lax.ppermute(value, axis, pairs)  14.2 us
    pallas_call x1, Pallas kernels, body(): pl.pallas_call(early_kernel, out_shape=[pltpu.VMEM((pivot_count * width,...  4.23 us
    pallas_call x1, Pallas kernels, body(): pl.pallas_call(late_kernel, out_shape=pltpu.VMEM((fields * SHARE_ROWS, LA...  3.19 us
    ppermute x4, waiting for transfers between devices, from_behind(): return lax.ppermute(value, axis, pairs)  2.37 us
    pallas_call x1, Pallas kernels, body(): pl.pallas_call(spread_kernel, out_shape=[jax.ShapeDtypeStruct((wide, pivo...  1.74 us
  transfers between devices with their start and end apart: 5, of which 1 were waited for; matrix products, arithmetic and copies ran while one was open for 0% of the time, Pallas kernels for 6%

profile of v3, /device:TPU:1, one launch (start us, length us, event | category | flops | bytes accessed | tf_op | source)
XLA Modules:
  0.0 78.3 jit_solution(7766109586386532848)
XLA Ops:
  0.0 0.0 copy-start
  0.0 1.7 %spread.1 = (f32[32,8,512]{2,1,0:T(8,128)}, f32[32,512]{1,0:T(8,128)S(1)}) custom-call(s32[8]{0:T(128)} %ids_ref.3, f32[32,512]{1,0:T(8,128)} %vectors_ref.1), custom_call_target="tpu_custom_call" | custom-call | tf_op jit(solution)/shard_map/spread/pallas_call | solution.py:247
  1.7 16.6 %all-to-all-start = ((f32[32,8,512]{2,1,0:T(8,128)}), f32[32,8,512]{2,1,0:T(8,128)S(1)}, u32[]{:S(2)}, u32[]{:S(2)}) async-start(f32[32,8,512]{2,1,0:T(8,128)} %get-tuple-element.13), calls=%async_computation | async-start | bytes 1048576 | tf_op jit(solution)/shard_map/all_to_all | solution.py:24
  18.4 3.1 %collective-permute-start = (f32[32,512]{1,0:T(8,128)S(1)}, f32[32,512]{1,0:T(8,128)S(1)}, u32[]{:S(2)}, u32[]{:S(2)}) collective-permute-start(f32[32,512]{1,0:T(8,128)S(1)} %get-tuple-element.12.own_ref), channel_id=1, source_target_pairs={{0,32},{32,64},{64,96},{96,128},{128,160},{160,192},{192,224},{224... | collective-permute-start | bytes 196616 | tf_op jit(solution)/shard_map/ppermute | solution.py:20
  21.5 4.0 %collective-permute-start.1 = (f32[32,512]{1,0:T(8,128)S(1)}, f32[32,512]{1,0:T(8,128)S(1)}, u32[]{:S(2)}, u32[]{:S(2)}) collective-permute-start(f32[32,512]{1,0:T(8,128)S(1)} %get-tuple-element.12.own_ref), channel_id=1, source_target_pairs={{0,64},{32,96},{64,128},{96,160},{128,192},{160,224},{192,256},{22... | collective-permute-start | bytes 196616 | tf_op jit(solution)/shard_map/ppermute | solution.py:20
  25.5 4.0 %collective-permute-start.2 = (f32[32,512]{1,0:T(8,128)S(1)}, f32[32,512]{1,0:T(8,128)S(1)}, u32[]{:S(2)}, u32[]{:S(2)}) collective-permute-start(f32[32,512]{1,0:T(8,128)S(1)} %get-tuple-element.12.own_ref), channel_id=1, source_target_pairs={{0,96},{32,128},{64,160},{96,192},{128,224},{160,256},{192,288},{2... | collective-permute-start | bytes 196616 | tf_op jit(solution)/shard_map/ppermute | solution.py:20
  29.5 3.1 %collective-permute-start.3 = (f32[32,512]{1,0:T(8,128)S(1)}, f32[32,512]{1,0:T(8,128)S(1)}, u32[]{:S(2)}, u32[]{:S(2)}) collective-permute-start(f32[32,512]{1,0:T(8,128)S(1)} %get-tuple-element.12.own_ref), channel_id=1, source_target_pairs={{0,128},{32,160},{64,192},{96,224},{128,256},{160,288},{192,320},{... | collective-permute-start | bytes 196616 | tf_op jit(solution)/shard_map/ppermute | solution.py:20
  32.6 0.6 turn.1.turned_ref
  33.2 2.4 %collective-permute-done.refs_0_ = f32[32,512]{1,0:T(8,128)S(1)} collective-permute-done((f32[32,512]{1,0:T(8,128)S(1)}, f32[32,512]{1,0:T(8,128)S(1)}, u32[]{:S(2)}, u32[]{:S(2)}) %collective-permute-start) | collective-permute-done | bytes 65568 | tf_op jit(solution)/shard_map/ppermute | solution.py:20
  35.6 0.0 collective-permute-done.1.refs_1_
  35.6 0.0 all-to-all-done.arrived_ref
  35.6 0.0 copy-done
  35.6 4.2 %early.1 = (f32[4096,128]{1,0:T(8,128)S(1)}, f32[64,128]{1,0:T(8,128)S(1)}, f32[8,128]{1,0:T(8,128)S(1)}, f32[128,128]{1,0:T(8,128)S(1)}, f32[16,128]{1,0:T(8,128)S(1)}) custom-call(s32[8]{0:T(128)S(1)} %copy-done, f32[32,512]{1,0:T(8,128)S(1)} %get-tuple-element.12.own_ref, f32[4096,128]{1,0:T(8,128)S(1)} %turn.1.turned_ref, ...), custom_call_target="tpu_custom_call" | custom-call | tf_op jit(solution)/shard_map/early/pallas_call | solution.py:270
  39.8 0.0 collective-permute-done.2.refs_0_
  39.8 0.0 collective-permute-done.3.refs_1_
  39.9 3.2 %late.1 = f32[320,128]{1,0:T(8,128)S(1)} custom-call(f32[4096,128]{1,0:T(8,128)S(1)} %turn.1.turned_ref, f32[4096,128]{1,0:T(8,128)S(1)} %get-tuple-element.14.splat_ref, f32[64,128]{1,0:T(8,128)S(1)} %get-tuple-element.15.smaller_ref, f32[8,128]{1,0:T(8,128)S(1)} %get-tuple-element.16.totals_ref, f32[128,128]{1,0:T(8,128)S(1)} %get-tuple-element.17.sums_ref, ...), custom_call_target="tpu_custom_call" | custom-call | tf_op jit(solution)/shard_map/late/pallas_call | solution.py:288
  43.0 34.4 %all_to_all.10 = f32[32,1,1280]{2,1,0:T(1,128)S(1)} all-to-all(f32[32,1,1280]{2,1,0:T(1,128)S(1)} %bitcast.4), channel_id=1, replica_groups=mesh['wide'=32,'fields'=32] {'fields'}, dimensions={0} | all-to-all | bytes 327680 | tf_op jit(solution)/shard_map/all_to_all | solution.py:24
  77.4 0.9 %quotient.1 = f32[4,8,32]{2,1,0:T(8,128)} custom-call(f32[320,128]{1,0:T(8,128)S(1)} %bitcast.3), custom_call_target="tpu_custom_call" | custom-call | tf_op jit(solution)/shard_map/quotient/pallas_call | solution.py:298
Async XLA Ops:
  0.0 35.6 %copy-start = (s32[8]{0:T(128)S(1)}, s32[8]{0:T(128)}, u32[]{:S(2)}) copy-start(s32[8]{0:T(128)} %ids_ref.3) | copy-start | bytes 100
  1.7 33.9 %all-to-all-start = ((f32[32,8,512]{2,1,0:T(8,128)}), f32[32,8,512]{2,1,0:T(8,128)S(1)}, u32[]{:S(2)}, u32[]{:S(2)}) async-start(f32[32,8,512]{2,1,0:T(8,128)} %get-tuple-element.13), calls=%async_computation | async-start | bytes 1048576 | tf_op jit(solution)/shard_map/all_to_all | solution.py:24
  18.4 17.2 %collective-permute-start = (f32[32,512]{1,0:T(8,128)S(1)}, f32[32,512]{1,0:T(8,128)S(1)}, u32[]{:S(2)}, u32[]{:S(2)}) collective-permute-start(f32[32,512]{1,0:T(8,128)S(1)} %get-tuple-element.12.own_ref), channel_id=1, source_target_pairs={{0,32},{32,64},{64,96},{96,128},{128,160},{160,192},{192,224},{224... | collective-permute-start | bytes 196616 | tf_op jit(solution)/shard_map/ppermute | solution.py:20
  21.5 14.1 %collective-permute-start.1 = (f32[32,512]{1,0:T(8,128)S(1)}, f32[32,512]{1,0:T(8,128)S(1)}, u32[]{:S(2)}, u32[]{:S(2)}) collective-permute-start(f32[32,512]{1,0:T(8,128)S(1)} %get-tuple-element.12.own_ref), channel_id=1, source_target_pairs={{0,64},{32,96},{64,128},{96,160},{128,192},{160,224},{192,256},{22... | collective-permute-start | bytes 196616 | tf_op jit(solution)/shard_map/ppermute | solution.py:20
  25.5 14.3 %collective-permute-start.2 = (f32[32,512]{1,0:T(8,128)S(1)}, f32[32,512]{1,0:T(8,128)S(1)}, u32[]{:S(2)}, u32[]{:S(2)}) collective-permute-start(f32[32,512]{1,0:T(8,128)S(1)} %get-tuple-element.12.own_ref), channel_id=1, source_target_pairs={{0,96},{32,128},{64,160},{96,192},{128,224},{160,256},{192,288},{2... | collective-permute-start | bytes 196616 | tf_op jit(solution)/shard_map/ppermute | solution.py:20
  29.5 10.3 %collective-permute-start.3 = (f32[32,512]{1,0:T(8,128)S(1)}, f32[32,512]{1,0:T(8,128)S(1)}, u32[]{:S(2)}, u32[]{:S(2)}) collective-permute-start(f32[32,512]{1,0:T(8,128)S(1)} %get-tuple-element.12.own_ref), channel_id=1, source_target_pairs={{0,128},{32,160},{64,192},{96,224},{128,256},{160,288},{192,320},{... | collective-permute-start | bytes 196616 | tf_op jit(solution)/shard_map/ppermute | solution.py:20

commit v4 on v3

--- a/solution.py
+++ b/solution.py
@@ -9,6 +9,7 @@
 STEPS = 4
 UNROLL = 32
 HALVES = 2
+ORDER = (1, 4), (2, 3)
 LANES = 128
 SUBLANES = 8
 SHARE_ROWS = SUBLANES + 2
@@ -75,8 +76,8 @@
             ).T
 
 
-def turn_partners(partner_refs, fields_ref):
-    row_count, width = partner_refs[0].shape
+def turn_partners(partners, fields_ref, row_count):
+    width = partners[0][0].shape[1]
     groups = row_count // SUBLANES
     for cp in range(groups // HALVES):
         for t in range(width // LANES):
@@ -84,7 +85,9 @@
             rows = []
             for h in range(HALVES):
                 first = (cp * HALVES + h) * SUBLANES
-                rows.extend([ref[first : first + SUBLANES, at] for ref in partner_refs] * groups)
+                rows.extend(
+                    [ref[base + first : base + first + SUBLANES, at] for ref, base in partners] * groups
+                )
             fields_ref[cp * width + t * LANES : cp * width + (t + 1) * LANES, :] = jnp.concatenate(
                 rows, axis=0
             ).T
@@ -129,7 +132,7 @@
     groups = row_count // SUBLANES
     for q in range(pivot_count):
         pivots_ref[q : q + 1, :] = arrived_ref[lax.div(ids_ref[q], row_count), q : q + 1, :]
-    turn_partners(partner_refs, fields_ref)
+    turn_partners([(ref, 0) for ref in partner_refs], fields_ref, row_count)
     for t in range(tiles):
         for q in range(pivot_count):
             splat_ref[q * width + t * LANES : q * width + (t + 1) * LANES, :] = jnp.broadcast_to(
@@ -167,15 +170,15 @@
         partners_ref[cp * SUBLANES : (cp + 1) * SUBLANES, :] = jnp.broadcast_to(row, (SUBLANES, LANES))
 
 
-def late_kernel(turned_ref, splat_ref, smaller_ref, totals_ref, sums_ref, partners_ref, *refs):
-    count = STEPS // HALVES
-    partner_refs = refs[:count]
-    out_ref, fields_ref = refs[count:]
-    row_count, width = partner_refs[0].shape
+def late_kernel(
+    turned_ref, splat_ref, smaller_ref, totals_ref, sums_ref, partners_ref, pair_ref, out_ref, fields_ref
+):
+    width = pair_ref.shape[1]
+    row_count = pair_ref.shape[0] // HALVES
     groups = row_count // SUBLANES
     pairs = groups // HALVES
     pivot_count = smaller_ref.shape[0] // SUBLANES
-    turn_partners(partner_refs, fields_ref)
+    turn_partners([(pair_ref, 0), (pair_ref, row_count)], fields_ref, row_count)
     smaller = [smaller_ref[q * SUBLANES : (q + 1) * SUBLANES, :] for q in range(pivot_count)]
     sums = sum_fields(turned_ref, splat_ref, fields_ref, smaller)
 
@@ -225,7 +228,7 @@
     ]
     turned = (1.5 * numerator / (by_group(columns * HALVES) + totals[0:1, :])).T
     for s in range(steps):
-        k, i = divmod(s, count)
+        k, i = next((k, half.index(s + 1)) for k, half in enumerate(ORDER) if s + 1 in half)
         rows = [(k * groups + g) * count * SUBLANES + i * SUBLANES for g in range(groups)]
         out_ref[s] = jnp.concatenate([turned[r : r + SUBLANES, :] for r in rows], axis=1)
 
@@ -256,9 +259,9 @@
         name="spread",
     )(pivot_ids, vectors)
     arrived = to_everyone(copies, "wide")
-    partners = []
-    for s in range(1, STEPS + 1):
-        partners.append(in_vmem(from_behind(vectors, "wide", s)))
+    behind = from_behind(vectors, "wide", 1)
+    pair = from_behind(jnp.concatenate([vectors, behind]), "wide", 2)
+    farthest = from_behind(vectors, "wide", STEPS)
     turned = pl.pallas_call(
         turn_kernel,
         out_shape=pltpu.VMEM((width * SUBLANES, LANES), jnp.float32),
@@ -278,22 +281,19 @@
         ],
         in_specs=[smem] + [vmem] * (3 + count),
         out_specs=[vmem] * 5,
-        scratch_shapes=[
-            pltpu.VMEM((pivot_count, width), jnp.float32),
-            pltpu.VMEM((pairs * width, LANES), jnp.float32),
-        ],
+        scratch_shapes=[pltpu.VMEM((pivot_count, width), jnp.float32), pltpu.VMEM((pairs * width, LANES), jnp.float32)],
         compiler_params=small,
         name="early",
-    )(pivot_ids, in_vmem(vectors), in_vmem(turned), in_vmem(arrived), *partners[:count])
+    )(pivot_ids, in_vmem(vectors), in_vmem(turned), *(in_vmem(a) for a in (arrived, behind, farthest)))
     table = pl.pallas_call(
         late_kernel,
         out_shape=pltpu.VMEM((fields * SHARE_ROWS, LANES), jnp.float32),
-        in_specs=[vmem] * (6 + count),
+        in_specs=[vmem] * 7,
         out_specs=vmem,
         scratch_shapes=[pltpu.VMEM((pairs * width, LANES), jnp.float32)],
         compiler_params=small,
         name="late",
-    )(in_vmem(turned), *(in_vmem(a) for a in between), *partners[count:])
+    )(in_vmem(turned), *(in_vmem(a) for a in (*between, pair)))
     shares = to_everyone(table.reshape(fields, 1, SHARE_ROWS * LANES), "fields")
     quotient = pl.pallas_call(
         quotient_kernel,

time: 78.7 us -> 85.4 us (1.085)
  waiting for transfers between devices: 2.37 us -> 16.8 us
  starting transfers between devices: 30.8 us -> 23.6 us
    ppermute x4 -> x3, waiting for transfers between devices: 2.37 us -> 16.8 us  [from_behind(): return lax.ppermute(value, axis, pairs)]
    ppermute x4 -> x3, starting transfers between devices: 14.2 us -> 7.01 us  [from_behind(): return lax.ppermute(value, axis, pairs)]
  transfers between devices with their start and end apart: 5 -> 4, of which waited for: 1 -> 2; matrix products, arithmetic and copies ran while one was open for 0% -> 0% of each run, Pallas kernels for 6% -> 6%
where the time goes in v4:
time: 85.4 us; the launch traced here: 85.1 us
  blocking collectives  33.9 us (40%)
  starting transfers between devices  23.6 us (28%)
  waiting for transfers between devices  16.8 us (20%)
  Pallas kernels  10.6 us (12%)
    all_to_all x1, blocking collectives, to_everyone(): return lax.all_to_all(copies, axis, split_axis=0, concat_axis=0, tiled=True)  33.9 us
    ppermute x3, waiting for transfers between devices, from_behind(): return lax.ppermute(value, axis, pairs)  16.8 us
    all_to_all x1, starting transfers between devices, to_everyone(): return lax.all_to_all(copies, axis, split_axis=0, concat_axis=0, tiled=True)  16.6 us
    ppermute x3, starting transfers between devices, from_behind(): return lax.ppermute(value, axis, pairs)  7.01 us
    pallas_call x1, Pallas kernels, body(): pl.pallas_call(early_kernel, out_shape=[pltpu.VMEM((pivot_count * width,...  4.23 us
    pallas_call x1, Pallas kernels, body(): pl.pallas_call(late_kernel, out_shape=pltpu.VMEM((fields * SHARE_ROWS, LA...  3.18 us
    pallas_call x1, Pallas kernels, body(): pl.pallas_call(spread_kernel, out_shape=[jax.ShapeDtypeStruct((wide, pivo...  1.72 us
  transfers between devices with their start and end apart: 4, of which 2 were waited for; matrix products, arithmetic and copies ran while one was open for 0% of the time, Pallas kernels for 6%

profile of v4, /device:TPU:1, one launch (start us, length us, event | category | flops | bytes accessed | tf_op | source)
XLA Modules:
  0.0 85.1 jit_solution(4824260635062215038)
XLA Ops:
  0.0 0.0 copy-start
  0.0 1.7 %spread.1 = (f32[32,8,512]{2,1,0:T(8,128)}, f32[32,512]{1,0:T(8,128)S(1)}) custom-call(s32[8]{0:T(128)} %ids_ref.3, f32[32,512]{1,0:T(8,128)} %vectors_ref.1), custom_call_target="tpu_custom_call" | custom-call | tf_op jit(solution)/shard_map/spread/pallas_call | solution.py:250
  1.7 16.6 %all-to-all-start = ((f32[32,8,512]{2,1,0:T(8,128)}), f32[32,8,512]{2,1,0:T(8,128)S(1)}, u32[]{:S(2)}, u32[]{:S(2)}) async-start(f32[32,8,512]{2,1,0:T(8,128)} %get-tuple-element.13), calls=%async_computation | async-start | bytes 1048576 | tf_op jit(solution)/shard_map/all_to_all | solution.py:25
  18.4 3.1 %collective-permute-start = (f32[32,512]{1,0:T(8,128)S(1)}, f32[32,512]{1,0:T(8,128)S(1)}, u32[]{:S(2)}, u32[]{:S(2)}) collective-permute-start(f32[32,512]{1,0:T(8,128)S(1)} %get-tuple-element.12.own_ref), channel_id=1, source_target_pairs={{0,32},{32,64},{64,96},{96,128},{128,160},{160,192},{192,224},{224... | collective-permute-start | bytes 196616 | tf_op jit(solution)/shard_map/ppermute | solution.py:21
  21.5 13.1 %collective-permute-done.refs_0_ = f32[32,512]{1,0:T(8,128)S(1)} collective-permute-done((f32[32,512]{1,0:T(8,128)S(1)}, f32[32,512]{1,0:T(8,128)S(1)}, u32[]{:S(2)}, u32[]{:S(2)}) %collective-permute-start) | collective-permute-done | bytes 65568 | tf_op jit(solution)/shard_map/ppermute | solution.py:21
  34.7 1.9 %collective-permute-start.2 = (f32[64,512]{1,0:T(8,128)S(1)}, f32[64,512]{1,0:T(8,128)S(1)}, u32[]{:S(2)}, u32[]{:S(2)}) collective-permute-start(f32[64,512]{1,0:T(8,128)S(1)} %pad_maximum_fusion), channel_id=1, source_target_pairs={{0,64},{32,96},{64,128},{96,160},{128,192},{160,224},{192,256},{22... | collective-permute-start | bytes 393224 | tf_op jit(solution)/shard_map/ppermute | solution.py:21
  36.6 1.9 %collective-permute-start.1 = (f32[32,512]{1,0:T(8,128)S(1)}, f32[32,512]{1,0:T(8,128)S(1)}, u32[]{:S(2)}, u32[]{:S(2)}) collective-permute-start(f32[32,512]{1,0:T(8,128)S(1)} %get-tuple-element.12.own_ref), channel_id=1, source_target_pairs={{0,128},{32,160},{64,192},{96,224},{128,256},{160,288},{192,320},{... | collective-permute-start | bytes 196616 | tf_op jit(solution)/shard_map/ppermute | solution.py:21
  38.6 0.6 turn.1.turned_ref
  39.2 3.7 %collective-permute-done.1.refs_1_ = f32[32,512]{1,0:T(8,128)S(1)} collective-permute-done((f32[32,512]{1,0:T(8,128)S(1)}, f32[32,512]{1,0:T(8,128)S(1)}, u32[]{:S(2)}, u32[]{:S(2)}) %collective-permute-start.1) | collective-permute-done | bytes 65568 | tf_op jit(solution)/shard_map/ppermute | solution.py:21
  42.9 0.0 all-to-all-done.arrived_ref
  42.9 0.0 copy-done
  42.9 4.2 %early.1 = (f32[4096,128]{1,0:T(8,128)S(1)}, f32[64,128]{1,0:T(8,128)S(1)}, f32[8,128]{1,0:T(8,128)S(1)}, f32[128,128]{1,0:T(8,128)S(1)}, f32[16,128]{1,0:T(8,128)S(1)}) custom-call(s32[8]{0:T(128)S(1)} %copy-done, f32[32,512]{1,0:T(8,128)S(1)} %get-tuple-element.12.own_ref, f32[4096,128]{1,0:T(8,128)S(1)} %turn.1.turned_ref, ...), custom_call_target="tpu_custom_call" | custom-call | tf_op jit(solution)/shard_map/early/pallas_call | solution.py:273
  47.1 0.0 collective-permute-done.2.pair_ref
  47.1 3.2 %late.1 = f32[320,128]{1,0:T(8,128)S(1)} custom-call(f32[4096,128]{1,0:T(8,128)S(1)} %turn.1.turned_ref, f32[4096,128]{1,0:T(8,128)S(1)} %get-tuple-element.14.splat_ref, f32[64,128]{1,0:T(8,128)S(1)} %get-tuple-element.15.smaller_ref, f32[8,128]{1,0:T(8,128)S(1)} %get-tuple-element.16.totals_ref, f32[128,128]{1,0:T(8,128)S(1)} %get-tuple-element.17.sums_ref, ...), custom_call_target="tpu_custom_call" | custom-call | tf_op jit(solution)/shard_map/late/pallas_call | solution.py:288
  50.3 33.9 %all_to_all.10 = f32[32,1,1280]{2,1,0:T(1,128)S(1)} all-to-all(f32[32,1,1280]{2,1,0:T(1,128)S(1)} %bitcast.4), channel_id=1, replica_groups=mesh['wide'=32,'fields'=32] {'fields'}, dimensions={0} | all-to-all | bytes 327680 | tf_op jit(solution)/shard_map/all_to_all | solution.py:25
  84.2 0.9 %quotient.1 = f32[4,8,32]{2,1,0:T(8,128)} custom-call(f32[320,128]{1,0:T(8,128)S(1)} %bitcast.3), custom_call_target="tpu_custom_call" | custom-call | tf_op jit(solution)/shard_map/quotient/pallas_call | solution.py:298
  (1 shorter events, 0.0 us)
Async XLA Ops:
  0.0 42.9 %copy-start = (s32[8]{0:T(128)S(1)}, s32[8]{0:T(128)}, u32[]{:S(2)}) copy-start(s32[8]{0:T(128)} %ids_ref.3) | copy-start | bytes 100
  1.7 41.1 %all-to-all-start = ((f32[32,8,512]{2,1,0:T(8,128)}), f32[32,8,512]{2,1,0:T(8,128)S(1)}, u32[]{:S(2)}, u32[]{:S(2)}) async-start(f32[32,8,512]{2,1,0:T(8,128)} %get-tuple-element.13), calls=%async_computation | async-start | bytes 1048576 | tf_op jit(solution)/shard_map/all_to_all | solution.py:25
  18.4 16.3 %collective-permute-start = (f32[32,512]{1,0:T(8,128)S(1)}, f32[32,512]{1,0:T(8,128)S(1)}, u32[]{:S(2)}, u32[]{:S(2)}) collective-permute-start(f32[32,512]{1,0:T(8,128)S(1)} %get-tuple-element.12.own_ref), channel_id=1, source_target_pairs={{0,32},{32,64},{64,96},{96,128},{128,160},{160,192},{192,224},{224... | collective-permute-start | bytes 196616 | tf_op jit(solution)/shard_map/ppermute | solution.py:21
  34.7 12.4 %collective-permute-start.2 = (f32[64,512]{1,0:T(8,128)S(1)}, f32[64,512]{1,0:T(8,128)S(1)}, u32[]{:S(2)}, u32[]{:S(2)}) collective-permute-start(f32[64,512]{1,0:T(8,128)S(1)} %pad_maximum_fusion), channel_id=1, source_target_pairs={{0,64},{32,96},{64,128},{96,160},{128,192},{160,224},{192,256},{22... | collective-permute-start | bytes 393224 | tf_op jit(solution)/shard_map/ppermute | solution.py:21
  36.6 6.2 %collective-permute-start.1 = (f32[32,512]{1,0:T(8,128)S(1)}, f32[32,512]{1,0:T(8,128)S(1)}, u32[]{:S(2)}, u32[]{:S(2)}) collective-permute-start(f32[32,512]{1,0:T(8,128)S(1)} %get-tuple-element.12.own_ref), channel_id=1, source_target_pairs={{0,128},{32,160},{64,192},{96,224},{128,256},{160,288},{192,320},{... | collective-permute-start | bytes 196616 | tf_op jit(solution)/shard_map/ppermute | solution.py:21

commit v5 on v2

--- a/solution.py
+++ b/solution.py
@@ -5,6 +5,7 @@
 from jax.experimental.pallas import tpu as pltpu
 from jax.sharding import PartitionSpec as P
 
+
 STEPS = 4
 UNROLL = 32
 LANES = 128
@@ -18,14 +19,26 @@
     return lax.ppermute(value, axis, pairs)
 
 
-def to_everyone(copies, axis):
-    return lax.all_to_all(copies, axis, split_axis=0, concat_axis=0, tiled=True)
-
-
-def spread_kernel(ids_ref, vectors_ref, copies_ref, rows_ref):
-    row_count = vectors_ref.shape[0]
+def to_everyone(copies, axis, groups=None):
+    return lax.all_to_all(
+        copies, axis, split_axis=0, concat_axis=0, tiled=True, axis_index_groups=groups
+    )
+
+
+def block_distance(ids_ref, q, row_count, behind, blocks):
+    return lax.rem(behind - lax.div(ids_ref[q], row_count) + blocks, blocks)
+
+
+def spread_kernel(ids_ref, place_ref, *refs):
+    held_refs = refs[:STEPS]
+    copies_ref, held_ref, rows_ref = refs[STEPS:]
+    row_count = held_refs[0].shape[0]
+    blocks = copies_ref.shape[0] * STEPS
+    for step, ref in enumerate(held_refs):
+        held_ref[step] = ref[...]
     for q in range(rows_ref.shape[0]):
-        rows_ref[q : q + 1, :] = vectors_ref[pl.ds(lax.rem(ids_ref[q], row_count), 1), :]
+        step = lax.min(block_distance(ids_ref, q, row_count, place_ref[0], blocks), STEPS - 1)
+        rows_ref[q : q + 1, :] = held_ref[step, pl.ds(lax.rem(ids_ref[q], row_count), 1), :]
     rows = rows_ref[...]
     for peer in range(copies_ref.shape[0]):
         copies_ref[peer] = rows
@@ -72,15 +85,20 @@
             turned_ref[pl.ds(t * LANES * SUBLANES + a, LANES, stride=SUBLANES), :] = rows.T
 
 
-def table_kernel(ids_ref, own_ref, turned_ref, arrived_ref, *refs):
+def table_kernel(ids_ref, place_ref, own_ref, turned_ref, arrived_ref, *refs):
     partner_refs = refs[:STEPS]
     out_ref, pivots_ref, fields_ref, splat_ref = refs[STEPS:]
     row_count, width = own_ref.shape
     pivot_count = pivots_ref.shape[0]
     tiles = width // LANES
     groups = row_count // SUBLANES
+    peers = arrived_ref.shape[0]
     for q in range(pivot_count):
-        pivots_ref[q : q + 1, :] = arrived_ref[lax.div(ids_ref[q], row_count), q : q + 1, :]
+        ahead = lax.div(
+            block_distance(ids_ref, q, row_count, place_ref[0], peers * STEPS), STEPS
+        )
+        peer = lax.rem(lax.div(place_ref[0], STEPS) - ahead + peers, peers)
+        pivots_ref[q : q + 1, :] = arrived_ref[peer, q : q + 1, :]
 
     for t in range(tiles):
         at = slice(t * LANES, (t + 1) * LANES)
@@ -180,35 +198,47 @@
     fields = lax.axis_size("fields")
     smem = pl.BlockSpec(memory_space=pltpu.SMEM)
     vmem = pl.BlockSpec(memory_space=pltpu.VMEM)
-    copies = pl.pallas_call(
-        spread_kernel,
-        out_shape=pltpu.VMEM((wide, pivot_count, width), jnp.float32),
-        in_specs=[smem, vmem],
-        out_specs=vmem,
-        scratch_shapes=[pltpu.VMEM((pivot_count, width), jnp.float32)],
-        name="spread",
-    )(pivot_ids, in_vmem(vectors))
-    arrived = to_everyone(copies, "wide")
-    partners = [from_behind(vectors, "wide", s) for s in range(1, STEPS + 1)]
+    small = pltpu.CompilerParams(vmem_limit_bytes=16 << 20)
+    peers = wide // STEPS
+    apart = [[first + STEPS * peer for peer in range(peers)] for first in range(STEPS)]
+    place = lax.axis_index("wide").astype(jnp.int32).reshape(1)
+    partners = []
+    for s in range(1, STEPS + 1):
+        partners.append(from_behind(vectors, "wide", s))
     turned = pl.pallas_call(
         turn_kernel,
         out_shape=pltpu.VMEM((width * SUBLANES, LANES), jnp.float32),
         in_specs=[vmem],
         out_specs=vmem,
+        compiler_params=small,
         name="turn",
     )(in_vmem(vectors))
+    copies = pl.pallas_call(
+        spread_kernel,
+        out_shape=jax.ShapeDtypeStruct((peers, pivot_count, width), jnp.float32),
+        in_specs=[smem] * 2 + [vmem] * STEPS,
+        out_specs=vmem,
+        scratch_shapes=[
+            pltpu.VMEM((STEPS, row_count, width), jnp.float32),
+            pltpu.VMEM((pivot_count, width), jnp.float32),
+        ],
+        compiler_params=small,
+        name="spread",
+    )(pivot_ids, place, *(in_vmem(a) for a in (vectors, *partners[:-1])))
+    arrived = to_everyone(copies, "wide", apart)
     table = pl.pallas_call(
         table_kernel,
         out_shape=pltpu.VMEM((fields * SHARE_ROWS, LANES), jnp.float32),
-        in_specs=[smem] + [vmem] * (3 + STEPS),
+        in_specs=[smem] * 2 + [vmem] * (3 + STEPS),
         out_specs=vmem,
         scratch_shapes=[
             pltpu.VMEM((pivot_count, width), jnp.float32),
             pltpu.VMEM((row_count // SUBLANES * width, LANES), jnp.float32),
             pltpu.VMEM((pivot_count * width, LANES), jnp.float32),
         ],
+        compiler_params=small,
         name="table",
-    )(pivot_ids, *(in_vmem(a) for a in (vectors, turned, arrived, *partners)))
+    )(pivot_ids, place, *(in_vmem(a) for a in (vectors, turned, arrived, *partners)))
     shares = to_everyone(table.reshape(fields, 1, SHARE_ROWS * LANES), "fields")
     quotient = pl.pallas_call(
         quotient_kernel,

time: 79.7 us -> 81.3 us (1.020)
  starting transfers between devices: 30 us -> 25.7 us
  waiting for transfers between devices: 6.85 us -> 10.5 us
  local copies, waits for them, and re-layouts: 0.84 us -> 2.34 us
  blocking collectives: 31.8 us -> 32.9 us
    all_to_all x1, starting transfers between devices: 16.6 us -> 6.9 us  [to_everyone(): lax.all_to_all(copies, axis, split_axis=0, concat_axis=0, tiled=True, axi...]
    ppermute x4, starting transfers between devices: 13.3 us -> 18.8 us  [from_behind(): return lax.ppermute(value, axis, pairs)]
    ppermute x4, waiting for transfers between devices: 6.84 us -> 8.97 us  [from_behind(): return lax.ppermute(value, axis, pairs)]
    all_to_all x1, waiting for transfers between devices: 0.01 us -> 1.52 us  [to_everyone(): lax.all_to_all(copies, axis, split_axis=0, concat_axis=0, tiled=True, axi...]
    unnamed x2 -> x10, local copies, waits for them, and re-layouts: 0.84 us -> 2.34 us
    all_to_all x1, blocking collectives: 31.8 us -> 32.9 us  [to_everyone(): lax.all_to_all(copies, axis, split_axis=0, concat_axis=0, tiled=True, axi...]
  transfers between devices with their start and end apart: 5 -> 5, of which waited for: 3 -> 4; matrix products, arithmetic and copies ran while one was open for 0% -> 0% of each run, Pallas kernels for 1% -> 1%
where the time goes in v5:
time: 81.3 us; the launch traced here: 80.8 us
  blocking collectives  32.9 us (40%)
  starting transfers between devices  25.7 us (32%)
  waiting for transfers between devices  10.5 us (13%)
  Pallas kernels  9.39 us (12%)
  local copies, waits for them, and re-layouts  2.34 us (3%)
    all_to_all x1, blocking collectives, to_everyone(): lax.all_to_all(copies, axis, split_axis=0, concat_axis=0, tiled=True, axi...  32.9 us
    ppermute x4, starting transfers between devices, from_behind(): return lax.ppermute(value, axis, pairs)  18.8 us
    ppermute x4, waiting for transfers between devices, from_behind(): return lax.ppermute(value, axis, pairs)  8.97 us
    all_to_all x1, starting transfers between devices, to_everyone(): lax.all_to_all(copies, axis, split_axis=0, concat_axis=0, tiled=True, axi...  6.9 us
    pallas_call x1, Pallas kernels, body(): pl.pallas_call(table_kernel, out_shape=pltpu.VMEM((fields * SHARE_ROWS, L...  6.62 us
    unnamed x10, local copies, waits for them, and re-layouts  2.34 us
  transfers between devices with their start and end apart: 5, of which 4 were waited for; matrix products, arithmetic and copies ran while one was open for 0% of the time, Pallas kernels for 1%

profile of v5, /device:TPU:1, one launch (start us, length us, event | category | flops | bytes accessed | tf_op | source)
XLA Modules:
  0.0 80.8 jit_solution(2670314085706927218)
XLA Ops:
  0.0 0.0 copy-start.4
  0.0 11.3 %collective-permute-start.2 = (f32[32,512]{1,0:T(8,128)}, f32[32,512]{1,0:T(8,128)S(1)}, u32[]{:S(2)}, u32[]{:S(2)}) collective-permute-start(f32[32,512]{1,0:T(8,128)} %own_ref.3), channel_id=1, source_target_pairs={{0,96},{32,128},{64,160},{96,192},{128,224},{160,256},{192,288},{2... | collective-permute-start | bytes 196616 | tf_op jit(solution)/shard_map/ppermute | solution.py:19
  11.3 1.9 %collective-permute-start.1 = (f32[32,512]{1,0:T(8,128)}, f32[32,512]{1,0:T(8,128)S(1)}, u32[]{:S(2)}, u32[]{:S(2)}) collective-permute-start(f32[32,512]{1,0:T(8,128)} %own_ref.3), channel_id=1, source_target_pairs={{0,64},{32,96},{64,128},{96,160},{128,192},{160,224},{192,256},{22... | collective-permute-start | bytes 196616 | tf_op jit(solution)/shard_map/ppermute | solution.py:19
  13.2 2.2 %collective-permute-start = (f32[32,512]{1,0:T(8,128)}, f32[32,512]{1,0:T(8,128)S(1)}, u32[]{:S(2)}, u32[]{:S(2)}) collective-permute-start(f32[32,512]{1,0:T(8,128)} %own_ref.3), channel_id=1, source_target_pairs={{0,32},{32,64},{64,96},{96,128},{128,160},{160,192},{192,224},{224... | collective-permute-start | bytes 196616 | tf_op jit(solution)/shard_map/ppermute | solution.py:19
  15.4 0.0 collective-permute-done.2.refs_3_.refs_2_
  15.4 4.7 %collective-permute-done.1.refs_2_.refs_1_ = f32[32,512]{1,0:T(8,128)S(1)} collective-permute-done((f32[32,512]{1,0:T(8,128)}, f32[32,512]{1,0:T(8,128)S(1)}, u32[]{:S(2)}, u32[]{:S(2)}) %collective-permute-start.1) | collective-permute-done | bytes 65568 | tf_op jit(solution)/shard_map/ppermute | solution.py:19
  20.1 2.6 %collective-permute-done.refs_1_.refs_0_ = f32[32,512]{1,0:T(8,128)S(1)} collective-permute-done((f32[32,512]{1,0:T(8,128)}, f32[32,512]{1,0:T(8,128)S(1)}, u32[]{:S(2)}, u32[]{:S(2)}) %collective-permute-start) | collective-permute-done | bytes 65568 | tf_op jit(solution)/shard_map/ppermute | solution.py:19
  22.7 0.0 copy-start
  22.7 0.8 %copy-done = f32[32,512]{1,0:T(8,128)S(1)} copy-done((f32[32,512]{1,0:T(8,128)S(1)}, f32[32,512]{1,0:T(8,128)}, u32[]{:S(2)}) %copy-start) | copy-done | bytes 65560
  23.6 0.0 copy-start.3
  23.6 0.7 copy-done.3
  24.2 0.0 copy-start.2
  24.2 1.3 %spread.1 = f32[8,8,512]{2,1,0:T(8,128)} custom-call(s32[8]{0:T(128)S(1)} %copy-done.3, s32[1]{0:T(128)} %bitcast.place_ref, f32[32,512]{1,0:T(8,128)S(1)} %copy-done, f32[32,512]{1,0:T(8,128)S(1)} %collective-permute-done.refs_1_.refs_0_, f32[32,512]{1,0:T(8,128)S(1)} %collective-permute-done.1.refs_2_.refs_1_, ...), custom_call_target="tpu_custom_call" | custom-call | tf_op jit(solution)/shard_map/spread/pallas_call | solution.py:216
  25.5 6.9 %all-to-all-start = ((f32[8,8,512]{2,1,0:T(8,128)}), f32[8,8,512]{2,1,0:T(8,128)S(1)}, u32[]{:S(2)}, u32[]{:S(2)}) async-start(f32[8,8,512]{2,1,0:T(8,128)} %spread.1), calls=%async_computation | async-start | bytes 262144 | tf_op jit(solution)/shard_map/all_to_all | solution.py:23
  32.4 3.4 %collective-permute-start.3 = (f32[32,512]{1,0:T(8,128)}, f32[32,512]{1,0:T(8,128)S(1)}, u32[]{:S(2)}, u32[]{:S(2)}) collective-permute-start(f32[32,512]{1,0:T(8,128)} %own_ref.3), channel_id=1, source_target_pairs={{0,128},{32,160},{64,192},{96,224},{128,256},{160,288},{192,320},{... | collective-permute-start | bytes 196616 | tf_op jit(solution)/shard_map/ppermute | solution.py:19
  35.8 0.0 copy-start.1
  35.8 0.8 %copy-done.1 = f32[32,512]{1,0:T(8,128)S(1)} copy-done((f32[32,512]{1,0:T(8,128)S(1)}, f32[32,512]{1,0:T(8,128)}, u32[]{:S(2)}) %copy-start.1) | copy-done | bytes 65560
  36.6 0.6 turn.1.turned_ref
  37.2 1.7 %collective-permute-done.3.refs_3_ = f32[32,512]{1,0:T(8,128)S(1)} collective-permute-done((f32[32,512]{1,0:T(8,128)}, f32[32,512]{1,0:T(8,128)S(1)}, u32[]{:S(2)}, u32[]{:S(2)}) %collective-permute-start.3) | collective-permute-done | bytes 65568 | tf_op jit(solution)/shard_map/ppermute | solution.py:19
  38.9 1.5 %all-to-all-done.arrived_ref = f32[8,8,512]{2,1,0:T(8,128)S(1)} async-done(((f32[8,8,512]{2,1,0:T(8,128)}), f32[8,8,512]{2,1,0:T(8,128)S(1)}, u32[]{:S(2)}, u32[]{:S(2)}) %all-to-all-start) | async-done | bytes 131104 | tf_op jit(solution)/shard_map/all_to_all | solution.py:23
  40.4 0.0 copy-done.4
  40.4 0.0 copy-done.2
  40.4 6.6 %table.1 = f32[288,128]{1,0:T(8,128)S(1)} custom-call(s32[8]{0:T(128)S(1)} %copy-done.4, s32[1]{0:T(128)} %bitcast.place_ref, f32[32,512]{1,0:T(8,128)S(1)} %copy-done.2, f32[4096,128]{1,0:T(8,128)S(1)} %turn.1.turned_ref, f32[8,8,512]{2,1,0:T(8,128)S(1)} %all-to-all-done.arrived_ref, f32[32,512]{1,0:T(8,128)S(1)} %collective-permute-done.refs_1_.refs_0_, ...), custom_call_target="tpu_custom_call" | custom-call | tf_op jit(solution)/shard_map/table/pallas_call | solution.py:229
  47.1 32.9 %all_to_all.10 = f32[32,1,1152]{2,1,0:T(1,128)S(1)} all-to-all(f32[32,1,1152]{2,1,0:T(1,128)S(1)} %bitcast.4), channel_id=1, replica_groups=mesh['wide'=32,'fields'=32] {'fields'}, dimensions={0} | all-to-all | bytes 294912 | tf_op jit(solution)/shard_map/all_to_all | solution.py:23
  79.9 0.9 %quotient.1 = f32[4,8,32]{2,1,0:T(8,128)} custom-call(f32[288,128]{1,0:T(8,128)S(1)} %bitcast.5), custom_call_target="tpu_custom_call" | custom-call | tf_op jit(solution)/shard_map/quotient/pallas_call | solution.py:243
Async XLA Ops:
  0.0 40.4 %copy-start.4 = (s32[8]{0:T(128)S(1)}, s32[8]{0:T(128)}, u32[]{:S(2)}) copy-start(s32[8]{0:T(128)} %ids_ref.3) | copy-start | bytes 100
  0.0 15.4 %collective-permute-start.2 = (f32[32,512]{1,0:T(8,128)}, f32[32,512]{1,0:T(8,128)S(1)}, u32[]{:S(2)}, u32[]{:S(2)}) collective-permute-start(f32[32,512]{1,0:T(8,128)} %own_ref.3), channel_id=1, source_target_pairs={{0,96},{32,128},{64,160},{96,192},{128,224},{160,256},{192,288},{2... | collective-permute-start | bytes 196616 | tf_op jit(solution)/shard_map/ppermute | solution.py:19
  11.3 8.8 %collective-permute-start.1 = (f32[32,512]{1,0:T(8,128)}, f32[32,512]{1,0:T(8,128)S(1)}, u32[]{:S(2)}, u32[]{:S(2)}) collective-permute-start(f32[32,512]{1,0:T(8,128)} %own_ref.3), channel_id=1, source_target_pairs={{0,64},{32,96},{64,128},{96,160},{128,192},{160,224},{192,256},{22... | collective-permute-start | bytes 196616 | tf_op jit(solution)/shard_map/ppermute | solution.py:19
  13.2 9.5 %collective-permute-start = (f32[32,512]{1,0:T(8,128)}, f32[32,512]{1,0:T(8,128)S(1)}, u32[]{:S(2)}, u32[]{:S(2)}) collective-permute-start(f32[32,512]{1,0:T(8,128)} %own_ref.3), channel_id=1, source_target_pairs={{0,32},{32,64},{64,96},{96,128},{128,160},{160,192},{192,224},{224... | collective-permute-start | bytes 196616 | tf_op jit(solution)/shard_map/ppermute | solution.py:19
  22.7 0.8 %copy-start = (f32[32,512]{1,0:T(8,128)S(1)}, f32[32,512]{1,0:T(8,128)}, u32[]{:S(2)}) copy-start(f32[32,512]{1,0:T(8,128)} %own_ref.3) | copy-start | bytes 196612
  23.6 0.7 copy-start.3
  24.2 16.2 %copy-start.2 = (f32[32,512]{1,0:T(8,128)S(1)}, f32[32,512]{1,0:T(8,128)}, u32[]{:S(2)}) copy-start(f32[32,512]{1,0:T(8,128)} %own_ref.3) | copy-start | bytes 196612
  25.5 14.9 %all-to-all-start = ((f32[8,8,512]{2,1,0:T(8,128)}), f32[8,8,512]{2,1,0:T(8,128)S(1)}, u32[]{:S(2)}, u32[]{:S(2)}) async-start(f32[8,8,512]{2,1,0:T(8,128)} %spread.1), calls=%async_computation | async-start | bytes 262144 | tf_op jit(solution)/shard_map/all_to_all | solution.py:23
  32.4 6.5 %collective-permute-start.3 = (f32[32,512]{1,0:T(8,128)}, f32[32,512]{1,0:T(8,128)S(1)}, u32[]{:S(2)}, u32[]{:S(2)}) collective-permute-start(f32[32,512]{1,0:T(8,128)} %own_ref.3), channel_id=1, source_target_pairs={{0,128},{32,160},{64,192},{96,224},{128,256},{160,288},{192,320},{... | collective-permute-start | bytes 196616 | tf_op jit(solution)/shard_map/ppermute | solution.py:19
  35.8 0.9 %copy-start.1 = (f32[32,512]{1,0:T(8,128)S(1)}, f32[32,512]{1,0:T(8,128)}, u32[]{:S(2)}) copy-start(f32[32,512]{1,0:T(8,128)} %own_ref.3) | copy-start | bytes 196612

commit v6 on v5

--- a/solution.py
+++ b/solution.py
@@ -85,9 +85,23 @@
             turned_ref[pl.ds(t * LANES * SUBLANES + a, LANES, stride=SUBLANES), :] = rows.T
 
 
-def table_kernel(ids_ref, place_ref, own_ref, turned_ref, arrived_ref, *refs):
+def partners_kernel(*refs):
     partner_refs = refs[:STEPS]
-    out_ref, pivots_ref, fields_ref, splat_ref = refs[STEPS:]
+    (fields_ref,) = refs[STEPS:]
+    row_count, width = partner_refs[0].shape
+    groups = row_count // SUBLANES
+    for t in range(width // LANES):
+        at = slice(t * LANES, (t + 1) * LANES)
+        for cg in range(groups):
+            rows = [ref[cg * SUBLANES : (cg + 1) * SUBLANES, at] for ref in partner_refs]
+            fields_ref[cg * width + t * LANES : cg * width + (t + 1) * LANES, :] = jnp.concatenate(
+                rows * groups, axis=0
+            ).T
+
+
+def table_kernel(
+    ids_ref, place_ref, own_ref, turned_ref, fields_ref, arrived_ref, out_ref, pivots_ref, splat_ref
+):
     row_count, width = own_ref.shape
     pivot_count = pivots_ref.shape[0]
     tiles = width // LANES
@@ -102,11 +116,6 @@
 
     for t in range(tiles):
         at = slice(t * LANES, (t + 1) * LANES)
-        for cg in range(groups):
-            rows = [ref[cg * SUBLANES : (cg + 1) * SUBLANES, at] for ref in partner_refs]
-            fields_ref[cg * width + t * LANES : cg * width + (t + 1) * LANES, :] = jnp.concatenate(
-                rows * groups, axis=0
-            ).T
         for q in range(pivot_count):
             splat_ref[q * width + t * LANES : q * width + (t + 1) * LANES, :] = jnp.broadcast_to(
                 pivots_ref[q : q + 1, at], (LANES, LANES)
@@ -226,19 +235,26 @@
         name="spread",
     )(pivot_ids, place, *(in_vmem(a) for a in (vectors, *partners[:-1])))
     arrived = to_everyone(copies, "wide", apart)
+    turned_partners = pl.pallas_call(
+        partners_kernel,
+        out_shape=pltpu.VMEM((row_count // SUBLANES * width, LANES), jnp.float32),
+        in_specs=[vmem] * STEPS,
+        out_specs=vmem,
+        compiler_params=small,
+        name="partners",
+    )(*(in_vmem(a) for a in partners))
     table = pl.pallas_call(
         table_kernel,
         out_shape=pltpu.VMEM((fields * SHARE_ROWS, LANES), jnp.float32),
-        in_specs=[smem] * 2 + [vmem] * (3 + STEPS),
+        in_specs=[smem] * 2 + [vmem] * 4,
         out_specs=vmem,
         scratch_shapes=[
             pltpu.VMEM((pivot_count, width), jnp.float32),
-            pltpu.VMEM((row_count // SUBLANES * width, LANES), jnp.float32),
             pltpu.VMEM((pivot_count * width, LANES), jnp.float32),
         ],
         compiler_params=small,
         name="table",
-    )(pivot_ids, place, *(in_vmem(a) for a in (vectors, turned, arrived, *partners)))
+    )(pivot_ids, place, *(in_vmem(a) for a in (vectors, turned, turned_partners, arrived)))
     shares = to_everyone(table.reshape(fields, 1, SHARE_ROWS * LANES), "fields")
     quotient = pl.pallas_call(
         quotient_kernel,

time: 81.3 us -> 81 us (level)
  no operation moved by 1% of the time
where the time goes in v6:
time: 81 us; the launch traced here: 80.6 us
  blocking collectives  32.9 us (41%)
  starting transfers between devices  25.7 us (32%)
  waiting for transfers between devices  10.2 us (13%)
  Pallas kernels  9.49 us (12%)
  local copies, waits for them, and re-layouts  2.34 us (3%)
    all_to_all x1, blocking collectives, to_everyone(): lax.all_to_all(copies, axis, split_axis=0, concat_axis=0, tiled=True, axi...  32.9 us
    ppermute x4, starting transfers between devices, from_behind(): return lax.ppermute(value, axis, pairs)  18.8 us
    ppermute x4, waiting for transfers between devices, from_behind(): return lax.ppermute(value, axis, pairs)  8.97 us
    all_to_all x1, starting transfers between devices, to_everyone(): lax.all_to_all(copies, axis, split_axis=0, concat_axis=0, tiled=True, axi...  6.9 us
    pallas_call x1, Pallas kernels, body(): pl.pallas_call(table_kernel, out_shape=pltpu.VMEM((fields * SHARE_ROWS, L...  6.39 us
    unnamed x10, local copies, waits for them, and re-layouts  2.34 us
  transfers between devices with their start and end apart: 5, of which 4 were waited for; matrix products, arithmetic and copies ran while one was open for 0% of the time, Pallas kernels for 1%

profile of v6, /device:TPU:1, one launch (start us, length us, event | category | flops | bytes accessed | tf_op | source)
XLA Modules:
  0.0 80.6 jit_solution(4396212937260754213)
XLA Ops:
  0.0 0.0 copy-start.4
  0.0 11.3 %collective-permute-start.2 = (f32[32,512]{1,0:T(8,128)}, f32[32,512]{1,0:T(8,128)S(1)}, u32[]{:S(2)}, u32[]{:S(2)}) collective-permute-start(f32[32,512]{1,0:T(8,128)} %own_ref.3), channel_id=1, source_target_pairs={{0,96},{32,128},{64,160},{96,192},{128,224},{160,256},{192,288},{2... | collective-permute-start | bytes 196616 | tf_op jit(solution)/shard_map/ppermute | solution.py:19
  11.3 1.9 %collective-permute-start.1 = (f32[32,512]{1,0:T(8,128)}, f32[32,512]{1,0:T(8,128)S(1)}, u32[]{:S(2)}, u32[]{:S(2)}) collective-permute-start(f32[32,512]{1,0:T(8,128)} %own_ref.3), channel_id=1, source_target_pairs={{0,64},{32,96},{64,128},{96,160},{128,192},{160,224},{192,256},{22... | collective-permute-start | bytes 196616 | tf_op jit(solution)/shard_map/ppermute | solution.py:19
  13.2 2.2 %collective-permute-start = (f32[32,512]{1,0:T(8,128)}, f32[32,512]{1,0:T(8,128)S(1)}, u32[]{:S(2)}, u32[]{:S(2)}) collective-permute-start(f32[32,512]{1,0:T(8,128)} %own_ref.3), channel_id=1, source_target_pairs={{0,32},{32,64},{64,96},{96,128},{128,160},{160,192},{192,224},{224... | collective-permute-start | bytes 196616 | tf_op jit(solution)/shard_map/ppermute | solution.py:19
  15.4 0.0 collective-permute-done.2.refs_2_.refs_3_
  15.4 4.7 %collective-permute-done.1.refs_1_.refs_2_ = f32[32,512]{1,0:T(8,128)S(1)} collective-permute-done((f32[32,512]{1,0:T(8,128)}, f32[32,512]{1,0:T(8,128)S(1)}, u32[]{:S(2)}, u32[]{:S(2)}) %collective-permute-start.1) | collective-permute-done | bytes 65568 | tf_op jit(solution)/shard_map/ppermute | solution.py:19
  20.1 2.6 %collective-permute-done.refs_0_.refs_1_ = f32[32,512]{1,0:T(8,128)S(1)} collective-permute-done((f32[32,512]{1,0:T(8,128)}, f32[32,512]{1,0:T(8,128)S(1)}, u32[]{:S(2)}, u32[]{:S(2)}) %collective-permute-start) | collective-permute-done | bytes 65568 | tf_op jit(solution)/shard_map/ppermute | solution.py:19
  22.7 0.0 copy-start
  22.7 0.8 %copy-done = f32[32,512]{1,0:T(8,128)S(1)} copy-done((f32[32,512]{1,0:T(8,128)S(1)}, f32[32,512]{1,0:T(8,128)}, u32[]{:S(2)}) %copy-start) | copy-done | bytes 65560
  23.6 0.0 copy-start.3
  23.6 0.7 copy-done.3
  24.2 0.0 copy-start.2
  24.2 1.3 %spread.1 = f32[8,8,512]{2,1,0:T(8,128)} custom-call(s32[8]{0:T(128)S(1)} %copy-done.3, s32[1]{0:T(128)} %bitcast.place_ref, f32[32,512]{1,0:T(8,128)S(1)} %copy-done, f32[32,512]{1,0:T(8,128)S(1)} %collective-permute-done.refs_0_.refs_1_, f32[32,512]{1,0:T(8,128)S(1)} %collective-permute-done.1.refs_1_.refs_2_, ...), custom_call_target="tpu_custom_call" | custom-call | tf_op jit(solution)/shard_map/spread/pallas_call | solution.py:225
  25.5 6.9 %all-to-all-start = ((f32[8,8,512]{2,1,0:T(8,128)}), f32[8,8,512]{2,1,0:T(8,128)S(1)}, u32[]{:S(2)}, u32[]{:S(2)}) async-start(f32[8,8,512]{2,1,0:T(8,128)} %spread.1), calls=%async_computation | async-start | bytes 262144 | tf_op jit(solution)/shard_map/all_to_all | solution.py:23
  32.4 3.4 %collective-permute-start.3 = (f32[32,512]{1,0:T(8,128)}, f32[32,512]{1,0:T(8,128)S(1)}, u32[]{:S(2)}, u32[]{:S(2)}) collective-permute-start(f32[32,512]{1,0:T(8,128)} %own_ref.3), channel_id=1, source_target_pairs={{0,128},{32,160},{64,192},{96,224},{128,256},{160,288},{192,320},{... | collective-permute-start | bytes 196616 | tf_op jit(solution)/shard_map/ppermute | solution.py:19
  35.8 0.0 copy-start.1
  35.8 0.8 %copy-done.1 = f32[32,512]{1,0:T(8,128)S(1)} copy-done((f32[32,512]{1,0:T(8,128)S(1)}, f32[32,512]{1,0:T(8,128)}, u32[]{:S(2)}) %copy-start.1) | copy-done | bytes 65560
  36.6 0.6 turn.1.turned_ref
  37.2 1.7 %collective-permute-done.3.refs_3_ = f32[32,512]{1,0:T(8,128)S(1)} collective-permute-done((f32[32,512]{1,0:T(8,128)}, f32[32,512]{1,0:T(8,128)S(1)}, u32[]{:S(2)}, u32[]{:S(2)}) %collective-permute-start.3) | collective-permute-done | bytes 65568 | tf_op jit(solution)/shard_map/ppermute | solution.py:19
  38.9 0.3 partners.1.fields_ref
  39.2 1.2 %all-to-all-done.arrived_ref = f32[8,8,512]{2,1,0:T(8,128)S(1)} async-done(((f32[8,8,512]{2,1,0:T(8,128)}), f32[8,8,512]{2,1,0:T(8,128)S(1)}, u32[]{:S(2)}, u32[]{:S(2)}) %all-to-all-start) | async-done | bytes 131104 | tf_op jit(solution)/shard_map/all_to_all | solution.py:23
  40.4 0.0 copy-done.4
  40.4 0.0 copy-done.2
  40.4 6.4 %table.1 = f32[288,128]{1,0:T(8,128)S(1)} custom-call(s32[8]{0:T(128)S(1)} %copy-done.4, s32[1]{0:T(128)} %bitcast.place_ref, f32[32,512]{1,0:T(8,128)S(1)} %copy-done.2, f32[4096,128]{1,0:T(8,128)S(1)} %turn.1.turned_ref, f32[2048,128]{1,0:T(8,128)S(1)} %partners.1.fields_ref, f32[8,8,512]{2,1,0:T(8,128)S(1)} %all-to-all-done.arrived_ref), custom_call_target="tpu_custom_call" | custom-call | tf_op jit(solution)/shard_map/table/pallas_call | solution.py:246
  46.8 32.9 %all_to_all.10 = f32[32,1,1152]{2,1,0:T(1,128)S(1)} all-to-all(f32[32,1,1152]{2,1,0:T(1,128)S(1)} %bitcast.4), channel_id=1, replica_groups=mesh['wide'=32,'fields'=32] {'fields'}, dimensions={0} | all-to-all | bytes 294912 | tf_op jit(solution)/shard_map/all_to_all | solution.py:23
  79.7 0.9 %quotient.1 = f32[4,8,32]{2,1,0:T(8,128)} custom-call(f32[288,128]{1,0:T(8,128)S(1)} %bitcast.5), custom_call_target="tpu_custom_call" | custom-call | tf_op jit(solution)/shard_map/quotient/pallas_call | solution.py:259
Async XLA Ops:
  0.0 40.4 %copy-start.4 = (s32[8]{0:T(128)S(1)}, s32[8]{0:T(128)}, u32[]{:S(2)}) copy-start(s32[8]{0:T(128)} %ids_ref.3) | copy-start | bytes 100
  0.0 15.4 %collective-permute-start.2 = (f32[32,512]{1,0:T(8,128)}, f32[32,512]{1,0:T(8,128)S(1)}, u32[]{:S(2)}, u32[]{:S(2)}) collective-permute-start(f32[32,512]{1,0:T(8,128)} %own_ref.3), channel_id=1, source_target_pairs={{0,96},{32,128},{64,160},{96,192},{128,224},{160,256},{192,288},{2... | collective-permute-start | bytes 196616 | tf_op jit(solution)/shard_map/ppermute | solution.py:19
  11.3 8.8 %collective-permute-start.1 = (f32[32,512]{1,0:T(8,128)}, f32[32,512]{1,0:T(8,128)S(1)}, u32[]{:S(2)}, u32[]{:S(2)}) collective-permute-start(f32[32,512]{1,0:T(8,128)} %own_ref.3), channel_id=1, source_target_pairs={{0,64},{32,96},{64,128},{96,160},{128,192},{160,224},{192,256},{22... | collective-permute-start | bytes 196616 | tf_op jit(solution)/shard_map/ppermute | solution.py:19
  13.2 9.5 %collective-permute-start = (f32[32,512]{1,0:T(8,128)}, f32[32,512]{1,0:T(8,128)S(1)}, u32[]{:S(2)}, u32[]{:S(2)}) collective-permute-start(f32[32,512]{1,0:T(8,128)} %own_ref.3), channel_id=1, source_target_pairs={{0,32},{32,64},{64,96},{96,128},{128,160},{160,192},{192,224},{224... | collective-permute-start | bytes 196616 | tf_op jit(solution)/shard_map/ppermute | solution.py:19
  22.7 0.8 %copy-start = (f32[32,512]{1,0:T(8,128)S(1)}, f32[32,512]{1,0:T(8,128)}, u32[]{:S(2)}) copy-start(f32[32,512]{1,0:T(8,128)} %own_ref.3) | copy-start | bytes 196612
  23.6 0.7 copy-start.3
  24.2 16.2 %copy-start.2 = (f32[32,512]{1,0:T(8,128)S(1)}, f32[32,512]{1,0:T(8,128)}, u32[]{:S(2)}) copy-start(f32[32,512]{1,0:T(8,128)} %own_ref.3) | copy-start | bytes 196612
  25.5 14.9 %all-to-all-start = ((f32[8,8,512]{2,1,0:T(8,128)}), f32[8,8,512]{2,1,0:T(8,128)S(1)}, u32[]{:S(2)}, u32[]{:S(2)}) async-start(f32[8,8,512]{2,1,0:T(8,128)} %spread.1), calls=%async_computation | async-start | bytes 262144 | tf_op jit(solution)/shard_map/all_to_all | solution.py:23
  32.4 6.5 %collective-permute-start.3 = (f32[32,512]{1,0:T(8,128)}, f32[32,512]{1,0:T(8,128)S(1)}, u32[]{:S(2)}, u32[]{:S(2)}) collective-permute-start(f32[32,512]{1,0:T(8,128)} %own_ref.3), channel_id=1, source_target_pairs={{0,128},{32,160},{64,192},{96,224},{128,256},{160,288},{192,320},{... | collective-permute-start | bytes 196616 | tf_op jit(solution)/shard_map/ppermute | solution.py:19
  35.8 0.9 %copy-start.1 = (f32[32,512]{1,0:T(8,128)S(1)}, f32[32,512]{1,0:T(8,128)}, u32[]{:S(2)}) copy-start(f32[32,512]{1,0:T(8,128)} %own_ref.3) | copy-start | bytes 196612

commit v7 on v5

--- a/solution.py
+++ b/solution.py
@@ -31,7 +31,7 @@
 
 def spread_kernel(ids_ref, place_ref, *refs):
     held_refs = refs[:STEPS]
-    copies_ref, held_ref, rows_ref = refs[STEPS:]
+    copies_ref, held_ref, rows_ref = refs[STEPS + 1 :]
     row_count = held_refs[0].shape[0]
     blocks = copies_ref.shape[0] * STEPS
     for step, ref in enumerate(held_refs):
@@ -215,8 +215,8 @@
     )(in_vmem(vectors))
     copies = pl.pallas_call(
         spread_kernel,
-        out_shape=jax.ShapeDtypeStruct((peers, pivot_count, width), jnp.float32),
-        in_specs=[smem] * 2 + [vmem] * STEPS,
+        out_shape=pltpu.VMEM((peers, pivot_count, width), jnp.float32),
+        in_specs=[smem] * 2 + [vmem] * (1 + STEPS),
         out_specs=vmem,
         scratch_shapes=[
             pltpu.VMEM((STEPS, row_count, width), jnp.float32),
@@ -224,7 +224,7 @@
         ],
         compiler_params=small,
         name="spread",
-    )(pivot_ids, place, *(in_vmem(a) for a in (vectors, *partners[:-1])))
+    )(pivot_ids, place, *(in_vmem(a) for a in (vectors, *partners)))
     arrived = to_everyone(copies, "wide", apart)
     table = pl.pallas_call(
         table_kernel,

time: 81.3 us -> 84 us (1.033)
  waiting for transfers between devices: 10.5 us -> 13.4 us
    all_to_all x1, waiting for transfers between devices: 1.52 us -> 6.53 us  [to_everyone(): lax.all_to_all(copies, axis, split_axis=0, concat_axis=0, tiled=True, axi...]
    ppermute x4, waiting for transfers between devices: 8.97 us -> 6.91 us  [from_behind(): return lax.ppermute(value, axis, pairs)]
  transfers between devices with their start and end apart: 5 -> 5, of which waited for: 4 -> 3; matrix products, arithmetic and copies ran while one was open for 0% -> 0% of each run, Pallas kernels for 1% -> 1%
where the time goes in v7:
time: 84 us; the launch traced here: 83.6 us
  blocking collectives  33.3 us (40%)
  starting transfers between devices  25.1 us (30%)
  waiting for transfers between devices  13.4 us (16%)
  Pallas kernels  9.39 us (11%)
  local copies, waits for them, and re-layouts  2.34 us (3%)
    all_to_all x1, blocking collectives, to_everyone(): lax.all_to_all(copies, axis, split_axis=0, concat_axis=0, tiled=True, axi...  33.3 us
    ppermute x4, starting transfers between devices, from_behind(): return lax.ppermute(value, axis, pairs)  18.7 us
    ppermute x4, waiting for transfers between devices, from_behind(): return lax.ppermute(value, axis, pairs)  6.91 us
    pallas_call x1, Pallas kernels, body(): pl.pallas_call(table_kernel, out_shape=pltpu.VMEM((fields * SHARE_ROWS, L...  6.62 us
    all_to_all x1, waiting for transfers between devices, to_everyone(): lax.all_to_all(copies, axis, split_axis=0, concat_axis=0, tiled=True, axi...  6.53 us
    all_to_all x1, starting transfers between devices, to_everyone(): lax.all_to_all(copies, axis, split_axis=0, concat_axis=0, tiled=True, axi...  6.38 us
    unnamed x10, local copies, waits for them, and re-layouts  2.34 us
  transfers between devices with their start and end apart: 5, of which 3 were waited for; matrix products, arithmetic and copies ran while one was open for 0% of the time, Pallas kernels for 1%

profile of v7, /device:TPU:1, one launch (start us, length us, event | category | flops | bytes accessed | tf_op | source)
XLA Modules:
  0.0 83.6 jit_solution(17009199468770765148)
XLA Ops:
  0.0 0.0 copy-start.4
  0.0 4.3 %collective-permute-start.3 = (f32[32,512]{1,0:T(8,128)}, f32[32,512]{1,0:T(8,128)S(1)}, u32[]{:S(2)}, u32[]{:S(2)}) collective-permute-start(f32[32,512]{1,0:T(8,128)} %own_ref.3), channel_id=1, source_target_pairs={{0,128},{32,160},{64,192},{96,224},{128,256},{160,288},{192,320},{... | collective-permute-start | bytes 196616 | tf_op jit(solution)/shard_map/ppermute | solution.py:19
  4.3 10.3 %collective-permute-start.2 = (f32[32,512]{1,0:T(8,128)}, f32[32,512]{1,0:T(8,128)S(1)}, u32[]{:S(2)}, u32[]{:S(2)}) collective-permute-start(f32[32,512]{1,0:T(8,128)} %own_ref.3), channel_id=1, source_target_pairs={{0,96},{32,128},{64,160},{96,192},{128,224},{160,256},{192,288},{2... | collective-permute-start | bytes 196616 | tf_op jit(solution)/shard_map/ppermute | solution.py:19
  14.6 1.9 %collective-permute-start.1 = (f32[32,512]{1,0:T(8,128)}, f32[32,512]{1,0:T(8,128)S(1)}, u32[]{:S(2)}, u32[]{:S(2)}) collective-permute-start(f32[32,512]{1,0:T(8,128)} %own_ref.3), channel_id=1, source_target_pairs={{0,64},{32,96},{64,128},{96,160},{128,192},{160,224},{192,256},{22... | collective-permute-start | bytes 196616 | tf_op jit(solution)/shard_map/ppermute | solution.py:19
  16.6 2.2 %collective-permute-start = (f32[32,512]{1,0:T(8,128)}, f32[32,512]{1,0:T(8,128)S(1)}, u32[]{:S(2)}, u32[]{:S(2)}) collective-permute-start(f32[32,512]{1,0:T(8,128)} %own_ref.3), channel_id=1, source_target_pairs={{0,32},{32,64},{64,96},{96,128},{128,160},{160,192},{192,224},{224... | collective-permute-start | bytes 196616 | tf_op jit(solution)/shard_map/ppermute | solution.py:19
  18.8 0.0 collective-permute-done.3.refs_4_.refs_3_
  18.8 0.0 collective-permute-done.2.refs_3_.refs_2_
  18.8 4.1 %collective-permute-done.1.refs_2_.refs_1_ = f32[32,512]{1,0:T(8,128)S(1)} collective-permute-done((f32[32,512]{1,0:T(8,128)}, f32[32,512]{1,0:T(8,128)S(1)}, u32[]{:S(2)}, u32[]{:S(2)}) %collective-permute-start.1) | collective-permute-done | bytes 65568 | tf_op jit(solution)/shard_map/ppermute | solution.py:19
  22.9 2.8 %collective-permute-done.refs_1_.refs_0_ = f32[32,512]{1,0:T(8,128)S(1)} collective-permute-done((f32[32,512]{1,0:T(8,128)}, f32[32,512]{1,0:T(8,128)S(1)}, u32[]{:S(2)}, u32[]{:S(2)}) %collective-permute-start) | collective-permute-done | bytes 65568 | tf_op jit(solution)/shard_map/ppermute | solution.py:19
  25.7 0.0 copy-start
  25.7 0.8 %copy-done = f32[32,512]{1,0:T(8,128)S(1)} copy-done((f32[32,512]{1,0:T(8,128)S(1)}, f32[32,512]{1,0:T(8,128)}, u32[]{:S(2)}) %copy-start) | copy-done | bytes 65560
  26.5 0.0 copy-start.3
  26.5 0.7 copy-done.3
  27.2 0.0 copy-start.2
  27.2 1.3 %spread.1 = f32[8,8,512]{2,1,0:T(8,128)} custom-call(s32[8]{0:T(128)S(1)} %copy-done.3, s32[1]{0:T(128)} %bitcast.place_ref, f32[32,512]{1,0:T(8,128)S(1)} %copy-done, f32[32,512]{1,0:T(8,128)S(1)} %collective-permute-done.refs_1_.refs_0_, f32[32,512]{1,0:T(8,128)S(1)} %collective-permute-done.1.refs_2_.refs_1_, ...), custom_call_target="tpu_custom_call" | custom-call | tf_op jit(solution)/shard_map/spread/pallas_call | solution.py:216
  28.4 6.4 %all-to-all-start = ((f32[8,8,512]{2,1,0:T(8,128)}), f32[8,8,512]{2,1,0:T(8,128)S(1)}, u32[]{:S(2)}, u32[]{:S(2)}) async-start(f32[8,8,512]{2,1,0:T(8,128)} %spread.1), calls=%async_computation | async-start | bytes 262144 | tf_op jit(solution)/shard_map/all_to_all | solution.py:23
  34.8 0.0 copy-start.1
  34.8 0.8 copy-done.1
  35.7 0.6 turn.1.turned_ref
  36.3 6.5 %all-to-all-done.arrived_ref = f32[8,8,512]{2,1,0:T(8,128)S(1)} async-done(((f32[8,8,512]{2,1,0:T(8,128)}), f32[8,8,512]{2,1,0:T(8,128)S(1)}, u32[]{:S(2)}, u32[]{:S(2)}) %all-to-all-start) | async-done | bytes 131104 | tf_op jit(solution)/shard_map/all_to_all | solution.py:23
  42.8 0.0 copy-done.4
  42.8 0.0 copy-done.2
  42.8 6.6 %table.1 = f32[288,128]{1,0:T(8,128)S(1)} custom-call(s32[8]{0:T(128)S(1)} %copy-done.4, s32[1]{0:T(128)} %bitcast.place_ref, f32[32,512]{1,0:T(8,128)S(1)} %copy-done.2, f32[4096,128]{1,0:T(8,128)S(1)} %turn.1.turned_ref, f32[8,8,512]{2,1,0:T(8,128)S(1)} %all-to-all-done.arrived_ref, f32[32,512]{1,0:T(8,128)S(1)} %collective-permute-done.refs_1_.refs_0_, ...), custom_call_target="tpu_custom_call" | custom-call | tf_op jit(solution)/shard_map/table/pallas_call | solution.py:229
  49.4 33.3 %all_to_all.10 = f32[32,1,1152]{2,1,0:T(1,128)S(1)} all-to-all(f32[32,1,1152]{2,1,0:T(1,128)S(1)} %bitcast.4), channel_id=1, replica_groups=mesh['wide'=32,'fields'=32] {'fields'}, dimensions={0} | all-to-all | bytes 294912 | tf_op jit(solution)/shard_map/all_to_all | solution.py:23
  82.7 0.9 %quotient.1 = f32[4,8,32]{2,1,0:T(8,128)} custom-call(f32[288,128]{1,0:T(8,128)S(1)} %bitcast.5), custom_call_target="tpu_custom_call" | custom-call | tf_op jit(solution)/shard_map/quotient/pallas_call | solution.py:243
Async XLA Ops:
  0.0 42.8 %copy-start.4 = (s32[8]{0:T(128)S(1)}, s32[8]{0:T(128)}, u32[]{:S(2)}) copy-start(s32[8]{0:T(128)} %ids_ref.3) | copy-start | bytes 100
  0.0 18.8 %collective-permute-start.3 = (f32[32,512]{1,0:T(8,128)}, f32[32,512]{1,0:T(8,128)S(1)}, u32[]{:S(2)}, u32[]{:S(2)}) collective-permute-start(f32[32,512]{1,0:T(8,128)} %own_ref.3), channel_id=1, source_target_pairs={{0,128},{32,160},{64,192},{96,224},{128,256},{160,288},{192,320},{... | collective-permute-start | bytes 196616 | tf_op jit(solution)/shard_map/ppermute | solution.py:19
  4.3 14.5 %collective-permute-start.2 = (f32[32,512]{1,0:T(8,128)}, f32[32,512]{1,0:T(8,128)S(1)}, u32[]{:S(2)}, u32[]{:S(2)}) collective-permute-start(f32[32,512]{1,0:T(8,128)} %own_ref.3), channel_id=1, source_target_pairs={{0,96},{32,128},{64,160},{96,192},{128,224},{160,256},{192,288},{2... | collective-permute-start | bytes 196616 | tf_op jit(solution)/shard_map/ppermute | solution.py:19
  14.6 8.2 %collective-permute-start.1 = (f32[32,512]{1,0:T(8,128)}, f32[32,512]{1,0:T(8,128)S(1)}, u32[]{:S(2)}, u32[]{:S(2)}) collective-permute-start(f32[32,512]{1,0:T(8,128)} %own_ref.3), channel_id=1, source_target_pairs={{0,64},{32,96},{64,128},{96,160},{128,192},{160,224},{192,256},{22... | collective-permute-start | bytes 196616 | tf_op jit(solution)/shard_map/ppermute | solution.py:19
  16.6 9.1 %collective-permute-start = (f32[32,512]{1,0:T(8,128)}, f32[32,512]{1,0:T(8,128)S(1)}, u32[]{:S(2)}, u32[]{:S(2)}) collective-permute-start(f32[32,512]{1,0:T(8,128)} %own_ref.3), channel_id=1, source_target_pairs={{0,32},{32,64},{64,96},{96,128},{128,160},{160,192},{192,224},{224... | collective-permute-start | bytes 196616 | tf_op jit(solution)/shard_map/ppermute | solution.py:19
  25.7 0.8 %copy-start = (f32[32,512]{1,0:T(8,128)S(1)}, f32[32,512]{1,0:T(8,128)}, u32[]{:S(2)}) copy-start(f32[32,512]{1,0:T(8,128)} %own_ref.3) | copy-start | bytes 196612
  26.5 0.7 copy-start.3
  27.2 15.6 %copy-start.2 = (f32[32,512]{1,0:T(8,128)S(1)}, f32[32,512]{1,0:T(8,128)}, u32[]{:S(2)}) copy-start(f32[32,512]{1,0:T(8,128)} %own_ref.3) | copy-start | bytes 196612
  28.4 14.4 %all-to-all-start = ((f32[8,8,512]{2,1,0:T(8,128)}), f32[8,8,512]{2,1,0:T(8,128)S(1)}, u32[]{:S(2)}, u32[]{:S(2)}) async-start(f32[8,8,512]{2,1,0:T(8,128)} %spread.1), calls=%async_computation | async-start | bytes 262144 | tf_op jit(solution)/shard_map/all_to_all | solution.py:23
  34.8 0.8 %copy-start.1 = (f32[32,512]{1,0:T(8,128)S(1)}, f32[32,512]{1,0:T(8,128)}, u32[]{:S(2)}) copy-start(f32[32,512]{1,0:T(8,128)} %own_ref.3) | copy-start | bytes 196612

commit v8 on v6

--- a/solution.py
+++ b/solution.py
@@ -114,12 +114,28 @@
         peer = lax.rem(lax.div(place_ref[0], STEPS) - ahead + peers, peers)
         pivots_ref[q : q + 1, :] = arrived_ref[peer, q : q + 1, :]
 
+    pivots = pivots_ref[...]
+    high = pivots.astype(jnp.bfloat16).astype(jnp.float32)
+    rest = pivots - high
+    middle = rest.astype(jnp.bfloat16).astype(jnp.float32)
+    parts = jnp.concatenate([high, middle, rest - middle, jnp.zeros_like(high)], axis=0)
+    parts = parts.astype(jnp.bfloat16)
+    shape = (parts.shape[0], pivot_count * LANES)
+    part = lax.broadcasted_iota(jnp.int32, shape, 0)
+    lane = lax.broadcasted_iota(jnp.int32, shape, 1)
+    chosen = jnp.where(lax.rem(part, pivot_count) == lax.div(lane, LANES), 1.0, 0.0)
+    chosen = chosen.astype(jnp.bfloat16)
     for t in range(tiles):
-        at = slice(t * LANES, (t + 1) * LANES)
+        splat = lax.dot_general(
+            parts[:, t * LANES : (t + 1) * LANES],
+            chosen,
+            (((0,), (0,)), ((), ())),
+            preferred_element_type=jnp.float32,
+        )
         for q in range(pivot_count):
-            splat_ref[q * width + t * LANES : q * width + (t + 1) * LANES, :] = jnp.broadcast_to(
-                pivots_ref[q : q + 1, at], (LANES, LANES)
-            ).T
+            splat_ref[q * width + t * LANES : q * width + (t + 1) * LANES, :] = splat[
+                :, q * LANES : (q + 1) * LANES
+            ]
 
     def some_fields(step, sums):
         sums = list(sums)

time: 81 us -> 80.9 us (level)
  no operation moved by 1% of the time
where the time goes in v8:
time: 80.9 us; the launch traced here: 80.4 us
  blocking collectives  32.9 us (41%)
  starting transfers between devices  25.7 us (32%)
  waiting for transfers between devices  10.2 us (13%)
  Pallas kernels  9.33 us (12%)
  local copies, waits for them, and re-layouts  2.34 us (3%)
    all_to_all x1, blocking collectives, to_everyone(): lax.all_to_all(copies, axis, split_axis=0, concat_axis=0, tiled=True, axi...  32.9 us
    ppermute x4, starting transfers between devices, from_behind(): return lax.ppermute(value, axis, pairs)  18.8 us
    ppermute x4, waiting for transfers between devices, from_behind(): return lax.ppermute(value, axis, pairs)  8.97 us
    all_to_all x1, starting transfers between devices, to_everyone(): lax.all_to_all(copies, axis, split_axis=0, concat_axis=0, tiled=True, axi...  6.9 us
    pallas_call x1, Pallas kernels, body(): pl.pallas_call(table_kernel, out_shape=pltpu.VMEM((fields * SHARE_ROWS, L...  6.23 us
    unnamed x10, local copies, waits for them, and re-layouts  2.34 us
  transfers between devices with their start and end apart: 5, of which 4 were waited for; matrix products, arithmetic and copies ran while one was open for 0% of the time, Pallas kernels for 1%

profile of v8, /device:TPU:1, one launch (start us, length us, event | category | flops | bytes accessed | tf_op | source)
XLA Modules:
  0.0 80.4 jit_solution(12383087471424724222)
XLA Ops:
  0.0 0.0 copy-start.4
  0.0 11.3 %collective-permute-start.2 = (f32[32,512]{1,0:T(8,128)}, f32[32,512]{1,0:T(8,128)S(1)}, u32[]{:S(2)}, u32[]{:S(2)}) collective-permute-start(f32[32,512]{1,0:T(8,128)} %own_ref.3), channel_id=1, source_target_pairs={{0,96},{32,128},{64,160},{96,192},{128,224},{160,256},{192,288},{2... | collective-permute-start | bytes 196616 | tf_op jit(solution)/shard_map/ppermute | solution.py:19
  11.3 1.9 %collective-permute-start.1 = (f32[32,512]{1,0:T(8,128)}, f32[32,512]{1,0:T(8,128)S(1)}, u32[]{:S(2)}, u32[]{:S(2)}) collective-permute-start(f32[32,512]{1,0:T(8,128)} %own_ref.3), channel_id=1, source_target_pairs={{0,64},{32,96},{64,128},{96,160},{128,192},{160,224},{192,256},{22... | collective-permute-start | bytes 196616 | tf_op jit(solution)/shard_map/ppermute | solution.py:19
  13.2 2.2 %collective-permute-start = (f32[32,512]{1,0:T(8,128)}, f32[32,512]{1,0:T(8,128)S(1)}, u32[]{:S(2)}, u32[]{:S(2)}) collective-permute-start(f32[32,512]{1,0:T(8,128)} %own_ref.3), channel_id=1, source_target_pairs={{0,32},{32,64},{64,96},{96,128},{128,160},{160,192},{192,224},{224... | collective-permute-start | bytes 196616 | tf_op jit(solution)/shard_map/ppermute | solution.py:19
  15.4 0.0 collective-permute-done.2.refs_2_.refs_3_
  15.4 4.7 %collective-permute-done.1.refs_1_.refs_2_ = f32[32,512]{1,0:T(8,128)S(1)} collective-permute-done((f32[32,512]{1,0:T(8,128)}, f32[32,512]{1,0:T(8,128)S(1)}, u32[]{:S(2)}, u32[]{:S(2)}) %collective-permute-start.1) | collective-permute-done | bytes 65568 | tf_op jit(solution)/shard_map/ppermute | solution.py:19
  20.1 2.6 %collective-permute-done.refs_0_.refs_1_ = f32[32,512]{1,0:T(8,128)S(1)} collective-permute-done((f32[32,512]{1,0:T(8,128)}, f32[32,512]{1,0:T(8,128)S(1)}, u32[]{:S(2)}, u32[]{:S(2)}) %collective-permute-start) | collective-permute-done | bytes 65568 | tf_op jit(solution)/shard_map/ppermute | solution.py:19
  22.7 0.0 copy-start
  22.7 0.8 %copy-done = f32[32,512]{1,0:T(8,128)S(1)} copy-done((f32[32,512]{1,0:T(8,128)S(1)}, f32[32,512]{1,0:T(8,128)}, u32[]{:S(2)}) %copy-start) | copy-done | bytes 65560
  23.6 0.0 copy-start.3
  23.6 0.7 copy-done.3
  24.2 0.0 copy-start.2
  24.2 1.3 %spread.1 = f32[8,8,512]{2,1,0:T(8,128)} custom-call(s32[8]{0:T(128)S(1)} %copy-done.3, s32[1]{0:T(128)} %bitcast.place_ref, f32[32,512]{1,0:T(8,128)S(1)} %copy-done, f32[32,512]{1,0:T(8,128)S(1)} %collective-permute-done.refs_0_.refs_1_, f32[32,512]{1,0:T(8,128)S(1)} %collective-permute-done.1.refs_1_.refs_2_, ...), custom_call_target="tpu_custom_call" | custom-call | tf_op jit(solution)/shard_map/spread/pallas_call | solution.py:241
  25.5 6.9 %all-to-all-start = ((f32[8,8,512]{2,1,0:T(8,128)}), f32[8,8,512]{2,1,0:T(8,128)S(1)}, u32[]{:S(2)}, u32[]{:S(2)}) async-start(f32[8,8,512]{2,1,0:T(8,128)} %spread.1), calls=%async_computation | async-start | bytes 262144 | tf_op jit(solution)/shard_map/all_to_all | solution.py:23
  32.4 3.4 %collective-permute-start.3 = (f32[32,512]{1,0:T(8,128)}, f32[32,512]{1,0:T(8,128)S(1)}, u32[]{:S(2)}, u32[]{:S(2)}) collective-permute-start(f32[32,512]{1,0:T(8,128)} %own_ref.3), channel_id=1, source_target_pairs={{0,128},{32,160},{64,192},{96,224},{128,256},{160,288},{192,320},{... | collective-permute-start | bytes 196616 | tf_op jit(solution)/shard_map/ppermute | solution.py:19
  35.8 0.0 copy-start.1
  35.8 0.8 %copy-done.1 = f32[32,512]{1,0:T(8,128)S(1)} copy-done((f32[32,512]{1,0:T(8,128)S(1)}, f32[32,512]{1,0:T(8,128)}, u32[]{:S(2)}) %copy-start.1) | copy-done | bytes 65560
  36.6 0.6 turn.1.turned_ref
  37.2 1.7 %collective-permute-done.3.refs_3_ = f32[32,512]{1,0:T(8,128)S(1)} collective-permute-done((f32[32,512]{1,0:T(8,128)}, f32[32,512]{1,0:T(8,128)S(1)}, u32[]{:S(2)}, u32[]{:S(2)}) %collective-permute-start.3) | collective-permute-done | bytes 65568 | tf_op jit(solution)/shard_map/ppermute | solution.py:19
  38.9 0.3 partners.1.fields_ref
  39.2 1.2 %all-to-all-done.arrived_ref = f32[8,8,512]{2,1,0:T(8,128)S(1)} async-done(((f32[8,8,512]{2,1,0:T(8,128)}), f32[8,8,512]{2,1,0:T(8,128)S(1)}, u32[]{:S(2)}, u32[]{:S(2)}) %all-to-all-start) | async-done | bytes 131104 | tf_op jit(solution)/shard_map/all_to_all | solution.py:23
  40.4 0.0 copy-done.4
  40.4 0.0 copy-done.2
  40.4 6.2 %table.1 = f32[288,128]{1,0:T(8,128)S(1)} custom-call(s32[8]{0:T(128)S(1)} %copy-done.4, s32[1]{0:T(128)} %bitcast.place_ref, f32[32,512]{1,0:T(8,128)S(1)} %copy-done.2, f32[4096,128]{1,0:T(8,128)S(1)} %turn.1.turned_ref, f32[2048,128]{1,0:T(8,128)S(1)} %partners.1.fields_ref, f32[8,8,512]{2,1,0:T(8,128)S(1)} %all-to-all-done.arrived_ref), custom_call_target="tpu_custom_call" | custom-call | tf_op jit(solution)/shard_map/table/pallas_call | solution.py:262
  46.7 32.9 %all_to_all.10 = f32[32,1,1152]{2,1,0:T(1,128)S(1)} all-to-all(f32[32,1,1152]{2,1,0:T(1,128)S(1)} %bitcast.4), channel_id=1, replica_groups=mesh['wide'=32,'fields'=32] {'fields'}, dimensions={0} | all-to-all | bytes 294912 | tf_op jit(solution)/shard_map/all_to_all | solution.py:23
  79.5 0.9 %quotient.1 = f32[4,8,32]{2,1,0:T(8,128)} custom-call(f32[288,128]{1,0:T(8,128)S(1)} %bitcast.5), custom_call_target="tpu_custom_call" | custom-call | tf_op jit(solution)/shard_map/quotient/pallas_call | solution.py:275
Async XLA Ops:
  0.0 40.4 %copy-start.4 = (s32[8]{0:T(128)S(1)}, s32[8]{0:T(128)}, u32[]{:S(2)}) copy-start(s32[8]{0:T(128)} %ids_ref.3) | copy-start | bytes 100
  0.0 15.4 %collective-permute-start.2 = (f32[32,512]{1,0:T(8,128)}, f32[32,512]{1,0:T(8,128)S(1)}, u32[]{:S(2)}, u32[]{:S(2)}) collective-permute-start(f32[32,512]{1,0:T(8,128)} %own_ref.3), channel_id=1, source_target_pairs={{0,96},{32,128},{64,160},{96,192},{128,224},{160,256},{192,288},{2... | collective-permute-start | bytes 196616 | tf_op jit(solution)/shard_map/ppermute | solution.py:19
  11.3 8.8 %collective-permute-start.1 = (f32[32,512]{1,0:T(8,128)}, f32[32,512]{1,0:T(8,128)S(1)}, u32[]{:S(2)}, u32[]{:S(2)}) collective-permute-start(f32[32,512]{1,0:T(8,128)} %own_ref.3), channel_id=1, source_target_pairs={{0,64},{32,96},{64,128},{96,160},{128,192},{160,224},{192,256},{22... | collective-permute-start | bytes 196616 | tf_op jit(solution)/shard_map/ppermute | solution.py:19
  13.2 9.5 %collective-permute-start = (f32[32,512]{1,0:T(8,128)}, f32[32,512]{1,0:T(8,128)S(1)}, u32[]{:S(2)}, u32[]{:S(2)}) collective-permute-start(f32[32,512]{1,0:T(8,128)} %own_ref.3), channel_id=1, source_target_pairs={{0,32},{32,64},{64,96},{96,128},{128,160},{160,192},{192,224},{224... | collective-permute-start | bytes 196616 | tf_op jit(solution)/shard_map/ppermute | solution.py:19
  22.7 0.8 %copy-start = (f32[32,512]{1,0:T(8,128)S(1)}, f32[32,512]{1,0:T(8,128)}, u32[]{:S(2)}) copy-start(f32[32,512]{1,0:T(8,128)} %own_ref.3) | copy-start | bytes 196612
  23.6 0.7 copy-start.3
  24.2 16.2 %copy-start.2 = (f32[32,512]{1,0:T(8,128)S(1)}, f32[32,512]{1,0:T(8,128)}, u32[]{:S(2)}) copy-start(f32[32,512]{1,0:T(8,128)} %own_ref.3) | copy-start | bytes 196612
  25.5 14.9 %all-to-all-start = ((f32[8,8,512]{2,1,0:T(8,128)}), f32[8,8,512]{2,1,0:T(8,128)S(1)}, u32[]{:S(2)}, u32[]{:S(2)}) async-start(f32[8,8,512]{2,1,0:T(8,128)} %spread.1), calls=%async_computation | async-start | bytes 262144 | tf_op jit(solution)/shard_map/all_to_all | solution.py:23
  32.4 6.5 %collective-permute-start.3 = (f32[32,512]{1,0:T(8,128)}, f32[32,512]{1,0:T(8,128)S(1)}, u32[]{:S(2)}, u32[]{:S(2)}) collective-permute-start(f32[32,512]{1,0:T(8,128)} %own_ref.3), channel_id=1, source_target_pairs={{0,128},{32,160},{64,192},{96,224},{128,256},{160,288},{192,320},{... | collective-permute-start | bytes 196616 | tf_op jit(solution)/shard_map/ppermute | solution.py:19
  35.8 0.9 %copy-start.1 = (f32[32,512]{1,0:T(8,128)S(1)}, f32[32,512]{1,0:T(8,128)}, u32[]{:S(2)}) copy-start(f32[32,512]{1,0:T(8,128)} %own_ref.3) | copy-start | bytes 196612
